TPU v7x, 128 devices: a whole 4x4x4 slice. The times are simulated.
128 devices in a mesh: seq: 8 (over y, core), head: 16 (over x, z).
Axes of the slice: x: 4, y: 4, z: 4, core: 2. Of those that a mesh axis runs over, the one named last changes fastest.
Arguments:
- queries: bfloat16 [16, 4096, 256], P('head', 'seq'), may hold values from -6 to 6
- keys: bfloat16 [2, 4096, 256], P(None, 'seq'), may hold values from -6 to 6
- values: bfloat16 [2, 4096, 256], P(None, 'seq'), may hold values from -6 to 6
- d_out: bfloat16 [16, 4096, 256], P('head', 'seq'), may hold values from -12 to 12
- doc_lengths: int32 [2, 8], replicated, may hold values from 1 to 1536, 4096 in all within a row
- fold_order: int32 [16], replicated, may hold values from 0 to 15, each once
Outputs:
- grad_queries: bfloat16 [16, 4096, 256], P('head', 'seq')
- grad_keys: float32 [2, 4096, 256], P(None, ('seq', 'head'))
- grad_values: float32 [2, 4096, 256], P(None, ('seq', 'head'))
Inputs may be any that keep to these rules, and one draw needn't show every extreme that they name: `doc_lengths`: each row's 8 lengths are at least 1, sum to 4096, and the longest is exactly 1536. fold_order names each of 0 to 15 once.
All inputs are finite; a program needn't handle non-finite values.
Results may differ from a plain program's by a relative error of at most 0.029.
Values may be sent and summed in bfloat16 or wider, within the bound.
A program may use at most 64 MiB of HBM per device.

v0:
```python
import jax
import jax.numpy as jnp
from jax import lax
from jax.sharding import PartitionSpec as P

HEAD_COUNT = 8


masked_value = -1e30


def sent_together(arrays, axis, split_dim, concat_dim, along):
    ends, at = ([], 0)
    for a in arrays[:-1]:
        at += a.shape[along]
        ends.append(at)
    both = jnp.concatenate(arrays, axis=along)
    return tuple(
        jnp.split(
            lax.all_to_all(both, axis, split_axis=split_dim, concat_axis=concat_dim, tiled=True),
            ends,
            axis=along,
        )
    )


def side_by_side(arrays, axis, dim, along):
    ends, at = ([], 0)
    for a in arrays[:-1]:
        at += a.shape[along]
        ends.append(at)
    both = jnp.concatenate(arrays, axis=along)
    return tuple(jnp.split(lax.all_gather(both, axis, axis=dim, tiled=True), ends, axis=along))


def side_by_side_2(arrays, axis, dim, along):
    ends, at = ([], 0)
    for a in arrays[:-1]:
        at += a.shape[along]
        ends.append(at)
    both = jnp.concatenate(arrays, axis=along)
    return tuple(
        jnp.split(lax.psum_scatter(both, axis, scatter_dimension=dim, tiled=True), ends, axis=along)
    )


def contract_last(left, right):
    return lax.dot_general(
        left, right, (((1,), (1,)), ((), ())), preferred_element_type=jnp.float32
    )


def contract_first(left, right):
    return lax.dot_general(
        left, right, (((0,), (0,)), ((), ())), preferred_element_type=jnp.float32
    )


def block_grads(query_rows, grad_out, log_norm, grad_dot, key_part, value_part, allowed, scaling):
    scores = contract_last(query_rows, key_part) * scaling
    weights = jnp.exp(jnp.where(allowed, scores - log_norm, masked_value))
    weights_low = weights.astype(jnp.bfloat16)
    grad_prob = contract_last(grad_out, value_part)
    grad_score = (weights * (grad_prob - grad_dot)).astype(jnp.bfloat16)
    part_query = jnp.dot(grad_score, key_part, preferred_element_type=jnp.float32) * scaling
    part_key = contract_first(grad_score, query_rows) * scaling
    part_value = contract_first(weights_low, grad_out)
    return (part_query, part_key, part_value)


def owner_blocks(key_part, value_part, row_count):
    head_total = lax.axis_size("head")
    piece_len = key_part.shape[0] // head_total
    width = key_part.shape[1]
    moved = tuple(
        (
            part.astype(jnp.float32)
            for part in sent_together(
                (key_part.astype(jnp.bfloat16), value_part.astype(jnp.bfloat16)), "head", 0, 0, 1
            )
        )
    )
    return tuple(
        (
            jnp.sum(item.reshape(row_count, head_total // row_count, piece_len, width), axis=1)
            for item in moved
        )
    )


def per_device(queries, keys, values, d_out, doc_lengths, fold_order):
    local_len = queries.shape[1]
    head_width = queries.shape[2]
    half_len = local_len // 2
    scaling = head_width ** (-0.5)
    seq_index = lax.axis_index("seq")
    row_index = lax.axis_index("head") // HEAD_COUNT
    row_count = keys.shape[0]
    span_ids = jnp.arange(fold_order.shape[0], dtype=jnp.int32)
    lengths = lax.dynamic_index_in_dim(doc_lengths, row_index, 0, keepdims=False)
    starts = jnp.cumsum(lengths, dtype=jnp.int32) - lengths

    def locate(indices):
        block_of = indices // half_len
        anchor = jnp.sum(
            jnp.where(block_of[:, None] == span_ids[None, :], fold_order[None, :], 0),
            axis=1,
            dtype=jnp.int32,
        )
        position = anchor * half_len + indices % half_len
        document = jnp.sum(
            (position[:, None] >= starts[None, :]).astype(jnp.int32), axis=1, dtype=jnp.int32
        )
        return (position, document)

    def allowed_pairs(query_place, key_place):
        return (query_place[1][:, None] == key_place[1][None, :]) & (
            key_place[0][None, :] <= query_place[0][:, None]
        )

    local_rows = jnp.arange(local_len, dtype=jnp.int32)
    own_place = locate(seq_index * local_len + local_rows)
    query_rows = queries[0]
    grad_out = d_out[0]
    key_row = lax.dynamic_index_in_dim(keys, row_index, 0, keepdims=False)
    value_row = lax.dynamic_index_in_dim(values, row_index, 0, keepdims=False)
    key_part, value_part = side_by_side((key_row, value_row), "seq", 0, 1)
    allowed = allowed_pairs(own_place, locate(jnp.arange(key_part.shape[0], dtype=jnp.int32)))
    run_max = jnp.full((local_len, 1), masked_value, jnp.float32)
    scores = jnp.where(allowed, contract_last(query_rows, key_part) * scaling, masked_value)
    new_max = jnp.maximum(run_max, jnp.max(scores, axis=1, keepdims=True))
    weights = jnp.where(allowed, jnp.exp(scores - new_max), 0.0)
    sum_next = jnp.sum(weights, axis=1, keepdims=True)
    acc_next = jnp.dot(weights.astype(jnp.bfloat16), value_part, preferred_element_type=jnp.float32)
    log_norm = new_max + jnp.log(sum_next)
    output = acc_next / sum_next
    grad_dot = jnp.sum(grad_out.astype(jnp.float32) * output, axis=1, keepdims=True)
    key_part, value_part = side_by_side((key_row, value_row), "seq", 0, 1)
    row_total = key_part.shape[0]
    allowed = allowed_pairs(own_place, locate(jnp.arange(row_total, dtype=jnp.int32)))
    part_query, part_key, part_value = block_grads(
        query_rows, grad_out, log_norm, grad_dot, key_part, value_part, allowed, scaling
    )
    full_keys = part_key
    full_values = part_value
    grad_query, full_keys, full_values = (part_query, full_keys, full_values)
    seq_keys, seq_values = tuple(
        (
            part.astype(jnp.float32)
            for part in side_by_side_2(
                (full_keys.astype(jnp.bfloat16), full_values.astype(jnp.bfloat16)), "seq", 0, 1
            )
        )
    )
    grad_keys, grad_values = owner_blocks(seq_keys, seq_values, row_count)
    grad_queries = grad_query.astype(jnp.bfloat16)[None]
    return (grad_queries, grad_keys, grad_values)


def solution(mesh):
    in_specs = (
        P("head", "seq", None),
        P(None, "seq", None),
        P(None, "seq", None),
        P("head", "seq", None),
        P(),
        P(),
    )
    out_specs = (
        P("head", "seq", None),
        P(None, ("seq", "head"), None),
        P(None, ("seq", "head"), None),
    )
    return jax.shard_map(
        per_device, mesh=mesh, in_specs=in_specs, out_specs=out_specs, check_vma=False
    )
```

profile of v0, /device:TPU:0, one launch (start us, length us, event | category | flops | bytes accessed | tf_op | source)
XLA Modules:
  0.0 138.8 jit_solution(12993161558894216928)
XLA Ops:
  7.2 1.1 dynamic-slice_bitcast_fusion
  8.3 0.8 pad_maximum_fusion.1
  9.2 0.7 constant_dynamic-slice_fusion
  9.9 0.2 reduce-window_clone.1
  10.1 1.1 copy.12
  11.2 0.7 select_reduce_fusion.1
  12.0 0.7 subtract_bitcast_fusion
  12.8 0.8 select_reduce_fusion
  13.7 30.6 %all-gather.2.cloned.1.call-done = bf16[4096,512]{1,0:T(8,128)(2,1)} async-done(((bf16[512,512]{1,0:T(8,128)(2,1)}), bf16[4096,512]{1,0:T(8,128)(2,1)}) %all-gather.2.cloned.1.call-update) | async-done | bytes 4194320 | tf_op jit(solution)/shard_map/all_gather | solution.py:33
  44.3 6.0 %fusion.3 = (f32[512]{0:T(512)S(1)}, f32[4096,512]{1,0:T(8,128)S(1)}) fusion(s32[512]{0:T(512)S(1)} %fusion.56, s32[4096]{0:T(1024)S(1)} %fusion.54, s32[4096]{0:T(1024)S(1)} %convert_reduce_fusion.2, s32[512]{0:T(512)S(1)} %convert_reduce_fusion.3, bf16[1,512,256]{2,1,0:T(8,128)(2,1)S(1)} %copy-done, bf16[4096,512]{1,0:T(8,128)(2,1)} %all-gather.2.cloned.1.call-done), kind=kOutput, calls=%fused_computation.8 | convolution fusion | flops 1086324224 | bytes 10786816 | tf_op jit(solution)/shard_map/dot_general | solution.py:48
  50.3 3.4 %fusion.7 = f32[512]{0:T(512)S(1)} fusion(f32[4096,512]{1,0:T(8,128)S(1)} %get-tuple-element.6, f32[512]{0:T(512)S(1)} %broadcast_maximum_fusion, s32[512]{0:T(512)S(1)} %fusion.56, s32[4096]{0:T(1024)S(1)} %fusion.54, s32[4096]{0:T(1024)S(1)} %convert_reduce_fusion.2, s32[512]{0:T(512)S(1)} %convert_reduce_fusion.3), kind=kLoop, calls=%fused_computation.14 | loop fusion | flops 16776704 | bytes 8429568 | tf_op jit(solution)/shard_map/reduce_sum | solution.py:133
  53.7 5.9 %convolution_convert_fusion = bf16[4096,256]{0,1:T(8,128)(2,1)S(1)} fusion(f32[4096,512]{1,0:T(8,128)S(1)} %get-tuple-element.6, f32[512]{0:T(512)S(1)} %log_add_fusion, bf16[1,512,256]{2,1,0:T(8,128)(2,1)S(1)} %copy-done.1, s32[512]{0:T(512)S(1)} %fusion.56, s32[512]{0:T(512)S(1)} %convert_reduce_fusion.3, s32[4096]{0:T(1024)S(1)} %fusion.54, ...), kind=kOutput, calls=%fused_computation.12 | convolution fusion | flops 1089470464 | bytes 10786816 | tf_op jit(solution)/shard_map/dot_general | solution.py:54
  59.6 3.2 %fusion.39 = f32[512]{0:T(512)S(1)} fusion(bf16[4096,512]{1,0:T(8,128)(2,1)S(1)} %copy-done.2, f32[4096,512]{1,0:T(8,128)S(1)} %get-tuple-element.6, f32[512]{0:T(512)S(1)} %broadcast_maximum_fusion, bf16[1,512,256]{1,2,0:T(8,128)(2,1)S(1)} %copy.12, f32[512]{0:T(512)S(1)} %fusion.7, s32[512]{0:T(512)S(1)} %fusion.56, s32[512]{0:T(512)S(1)} %convert_reduce_fusion.3, ...), kind=kOutput, calls=%fused_computation.31 | convolution fusion | flops 1091042816 | bytes 10790912 | tf_op jit(solution)/shard_map/dot_general | solution.py:134
  62.9 4.9 %fusion = bf16[512,4096]{0,1:T(8,128)(2,1)S(1)} fusion(f32[4096,512]{1,0:T(8,128)S(1)} %get-tuple-element.6, f32[512]{0:T(512)S(1)} %fusion.39, f32[512]{0:T(512)S(1)} %log_add_fusion, bf16[4096,512]{1,0:T(8,128)(2,1)S(1)} %copy-done.2, bf16[1,512,256]{2,1,0:T(8,128)(2,1)S(1)} %copy-done.1, s32[512]{0:T(512)S(1)} %fusion.56, s32[4096]{0:T(1024)S(1)} %fusion.54, ...), kind=kOutput, calls=%fused_computation.1 | convolution fusion | flops 1092616192 | bytes 14983168 | tf_op jit(solution)/shard_map/dot_general | solution.py:48
  67.7 2.0 %copy-done.3 = bf16[512,4096]{0,1:T(8,128)(2,1)} copy-done((bf16[512,4096]{0,1:T(8,128)(2,1)}, bf16[512,4096]{0,1:T(8,128)(2,1)S(1)}, u32[]{:S(2)}) %copy-start.3) | copy-done | bytes 4194328
  69.7 1.3 fusion.5
  71.0 2.5 %pad_maximum_fusion = bf16[4096,512]{0,1:T(8,128)(2,1)} fusion(bf16[4096,256]{0,1:T(8,128)(2,1)S(1)} %convolution_convert_fusion, bf16[4096,256]{0,1:T(8,128)(2,1)S(1)} %fusion.5), kind=kLoop, calls=%fused_computation.15 | loop fusion | flops 8388608 | bytes 8388608 | tf_op jit(solution)/shard_map/concatenate | solution.py:41
  73.5 38.1 %reduce-scatter.2.cloned.1.call-done = bf16[512,512]{0,1:T(8,128)(2,1)} async-done(((bf16[4096,512]{0,1:T(8,128)(2,1)}), bf16[512,512]{0,1:T(8,128)(2,1)}) %reduce-scatter.2.cloned.1.call-update) | async-done | bytes 524304 | tf_op jit(solution)/shard_map/reduce_scatter | solution.py:43
  111.6 2.1 %copy.13 = bf16[512,512]{1,0:T(8,128)(2,1)} copy(bf16[512,512]{0,1:T(8,128)(2,1)} %reduce-scatter.2.cloned.1.call-done) | data formatting | bytes 1048576 | tf_op jit(solution)/shard_map/reduce_scatter | solution.py:43
  113.7 6.9 %all-to-all-start = ((bf16[16,32,512]{2,1,0:T(8,128)(2,1)}), bf16[16,32,512]{2,1,0:T(8,128)(2,1)S(1)}, u32[]{:S(2)}, u32[]{:S(2)}) async-start(bf16[16,32,512]{2,1,0:T(8,128)(2,1)} %bitcast.8), calls=%async_computation.1 | async-start | bytes 1048576 | tf_op jit(solution)/shard_map/all_to_all | solution.py:20
  120.5 4.9 %fusion.26 = bf16[1,512,256]{2,1,0:T(8,128)(2,1)} fusion(bf16[512,4096]{0,1:T(8,128)(2,1)} %copy-done.3, bf16[4096,512]{1,0:T(8,128)(2,1)} %all-gather.2.cloned.1.call-done), kind=kOutput, calls=%fused_computation.28 | convolution fusion | flops 1074003968 | bytes 6553600 | tf_op jit(solution)/shard_map/dot_general | solution.py:65
  125.4 5.2 %all-to-all-done = bf16[16,32,512]{2,1,0:T(8,128)(2,1)S(1)} async-done(((bf16[16,32,512]{2,1,0:T(8,128)(2,1)}), bf16[16,32,512]{2,1,0:T(8,128)(2,1)S(1)}, u32[]{:S(2)}, u32[]{:S(2)}) %all-to-all-start) | async-done | bytes 524320 | tf_op jit(solution)/shard_map/all_to_all | solution.py:20
  130.7 0.7 convert_reduce_fusion.1
  131.3 0.7 convert_reduce_fusion
  (20 shorter events, 0.4 us)
Async XLA Ops:
  7.2 37.1 %copy-start = (bf16[1,512,256]{2,1,0:T(8,128)(2,1)S(1)}, bf16[1,512,256]{2,1,0:T(8,128)(2,1)}, u32[]{:S(2)}) copy-start(bf16[1,512,256]{2,1,0:T(8,128)(2,1)} %param.6) | copy-start | bytes 786436
  7.2 37.1 %all-gather.2.cloned.1.call-start = ((), (), s32[]{:S(2)}) async-start(), calls=%async_computation.2 | async-start | bytes 4718592 | tf_op jit(solution)/shard_map/all_gather | solution.py:33
  9.2 102.4 %reduce-scatter.2.cloned.1.call-start = ((), (), s32[]{:S(2)}) async-start(), calls=%async_computation.3 | async-start | bytes 4718592 | tf_op jit(solution)/shard_map/reduce_scatter | solution.py:43
  50.3 3.4 %copy-start.1 = (bf16[1,512,256]{2,1,0:T(8,128)(2,1)S(1)}, bf16[1,512,256]{2,1,0:T(8,128)(2,1)}, u32[]{:S(2)}) copy-start(bf16[1,512,256]{2,1,0:T(8,128)(2,1)} %param.9) | copy-start | bytes 786436
  53.7 5.9 %copy-start.2 = (bf16[4096,512]{1,0:T(8,128)(2,1)S(1)}, bf16[4096,512]{1,0:T(8,128)(2,1)}, u32[]{:S(2)}) copy-start(bf16[4096,512]{1,0:T(8,128)(2,1)} %all-gather.2.cloned.1.call-done) | copy-start | bytes 12582916
  67.7 2.0 %copy-start.3 = (bf16[512,4096]{0,1:T(8,128)(2,1)}, bf16[512,4096]{0,1:T(8,128)(2,1)S(1)}, u32[]{:S(2)}) copy-start(bf16[512,4096]{0,1:T(8,128)(2,1)S(1)} %fusion) | copy-start | bytes 12582916
  113.7 17.0 %all-to-all-start = ((bf16[16,32,512]{2,1,0:T(8,128)(2,1)}), bf16[16,32,512]{2,1,0:T(8,128)(2,1)S(1)}, u32[]{:S(2)}, u32[]{:S(2)}) async-start(bf16[16,32,512]{2,1,0:T(8,128)(2,1)} %bitcast.8), calls=%async_computation.1 | async-start | bytes 1048576 | tf_op jit(solution)/shard_map/all_to_all | solution.py:20
Sparse Core Ops, SparseCore 0:
  9.7 34.5 all-gather.1
  73.6 37.9 reduce-scatter.1
where the time goes:
time: 139 us
  waiting for transfers between devices  74 us (53%)
  matrix products  26.1 us (19%)
  between operations  14.2 us (10%)
  other arithmetic  10.7 us (8%)
  local copies, waits for them, and re-layouts  6.96 us (5%)
  starting transfers between devices  6.94 us (5%)
    reduce_scatter x1, waiting for transfers between devices, side_by_side_2(): lax.psum_scatter(both, axis, scatter_dimension=dim, tiled=True)  38.1 us
    all_gather x1, waiting for transfers between devices, side_by_side(): lax.all_gather(both, axis, axis=dim, tiled=True)  30.6 us
    dot_general x2, matrix products, contract_last(): lax.dot_general(left, right, (((1,), (1,)), ((), ())), preferred_element_...  10.8 us
    dot_general x2, matrix products, contract_first(): lax.dot_general(left, right, (((0,), (0,)), ((), ())), preferred_element_...  7.18 us
    all_to_all x1, starting transfers between devices, sent_together(): lax.all_to_all(both, axis, split_axis=split_dim, concat_axis=concat_dim,...  6.86 us
    all_to_all x1, waiting for transfers between devices, sent_together(): lax.all_to_all(both, axis, split_axis=split_dim, concat_axis=concat_dim,...  5.22 us
    dot_general x1, matrix products, block_grads(): jnp.dot(grad_score, key_part, preferred_element_type=jnp.float32) * scaling  4.87 us
    reduce_sum x1, other arithmetic, per_device(): sum_next = jnp.sum(weights, axis=1, keepdims=True)  3.39 us
  transfers between devices with their start and end apart: 3, of which 3 were waited for; matrix products, arithmetic and copies ran while one was open for 7% of the time, Pallas kernels for 0%

commit v1 on v0

v1 whole, which is shorter than its diff:
```python
import jax
import jax.numpy as jnp
from jax import lax
from jax.experimental import pallas as pl
from jax.experimental.pallas import tpu as pltpu
from jax.sharding import PartitionSpec as P

MESH = pl.DeviceIdType.MESH
LOG2E = 1.4426950408889634
MASKED = -1e30
BLOCK = 256
F32 = jnp.float32
BF16 = jnp.bfloat16
ROW_HEADS = 8
COPIES = 112


def nt(a, b):
    return lax.dot_general(a, b, (((1,), (1,)), ((), ())), preferred_element_type=F32)


def nn(a, b):
    return lax.dot_general(a, b, (((1,), (0,)), ((), ())), preferred_element_type=F32)


def tn(a, b):
    return lax.dot_general(a, b, (((0,), (0,)), ((), ())), preferred_element_type=F32)


def kernel(
    lengths, fold, q_hbm, k_hbm, v_hbm, do_hbm,
    dq_out, dk_out, dv_out,
    qv, dov, qs, kv, sc, dp, stat, dqt, dqo,
    psend, precv, ak, av, rk, fk, rv, fv, zv, ev, fev, yk, gk, fgk, xs, rx, dkv_out,
    local_sem, send_sem, recv_sem,
):
    s = lax.axis_index("seq")
    h = lax.axis_index("head")
    y, c = lax.div(s, 2), lax.rem(s, 2)
    x, z = lax.div(h, 4), lax.rem(h, 4)
    row = lax.div(h, ROW_HEADS)

    def around(v, k):
        return lax.rem(v + (k % 4), 4)

    partner = {"seq": 2 * y + (1 - c), "head": h}
    yp = {"seq": 2 * around(y, 1) + c, "head": h}
    ym = {"seq": 2 * around(y, -1) + c, "head": h}
    zp = {"seq": s, "head": 4 * x + around(z, 1)}
    zm = {"seq": s, "head": 4 * x + around(z, -1)}
    xo = [{"seq": s, "head": 4 * around(x, k) + z} for k in (1, 2, 3)]

    loads = [
        pltpu.make_async_copy(v_hbm.at[row], kv.at[s, 1], local_sem.at[0]),
        pltpu.make_async_copy(k_hbm.at[row], kv.at[s, 0], local_sem.at[1]),
        pltpu.make_async_copy(q_hbm.at[0], qv, local_sem.at[2]),
        pltpu.make_async_copy(do_hbm.at[0], dov, local_sem.at[3]),
    ]
    for cp in loads:
        cp.start()

    barrier = pltpu.get_barrier_semaphore()
    peers = [partner, yp, ym, zp, zm] + xo
    for peer in peers:
        pl.semaphore_signal(barrier, inc=1, device_id=peer, device_id_type=MESH)
    pl.semaphore_wait(barrier, len(peers))

    started = []

    def send(src, dst, device):
        i = len(started)
        cp = pltpu.make_async_remote_copy(
            src_ref=src, dst_ref=dst, send_sem=send_sem.at[i], recv_sem=recv_sem.at[i],
            device_id=device, device_id_type=MESH,
        )
        cp.start()
        started.append(cp)
        return cp

    def same(ref, device):
        return send(ref, ref, device)

    def sid(k, core):
        return 2 * around(y, k) + core

    other = 1 - c
    zq = 128 * z

    def vquarter(sidx, zi, lo, n):
        return kv.at[sidx, 1, pl.ds(pl.multiple_of(128 * zi + lo, 64), n)]

    loads[0].wait()
    va_p = same(vquarter(s, z, 0, 64), yp)
    vb_m = same(vquarter(s, z, 64, 64), ym)
    vb_p = same(vquarter(s, z, 64, 64), yp)
    va_m = same(vquarter(s, z, 0, 64), ym)
    loads[1].wait()
    ka_p = same(kv.at[s, 0, pl.ds(0, 256)], yp)
    kb_m = same(kv.at[s, 0, pl.ds(256, 256)], ym)
    kb_p = same(kv.at[s, 0, pl.ds(256, 256)], yp)
    ka_m = same(kv.at[s, 0, pl.ds(0, 256)], ym)
    own_pair = same(kv.at[s], partner)

    lane = lax.broadcasted_iota(jnp.int32, (1, 512), 1)
    base0 = fold[2 * s] * BLOCK
    base1 = fold[2 * s + 1] * BLOCK
    pos = jnp.where(lane < BLOCK, base0 + lane, base1 + lane - BLOCK)
    first = jnp.zeros((1, 512), jnp.int32)
    at = jnp.int32(0)
    for d in range(8):
        first = jnp.where(pos >= at, at, first)
        at = at + lengths[row, d]
    loads[2].wait()
    loads[3].wait()
    qs[...] = (qv[...].astype(F32) * 0.0625).astype(BF16)
    stat[0:1, :] = jnp.full((1, 512), MASKED, F32)
    stat[1:2, :] = jnp.zeros((1, 512), F32)
    stat[2:3, :] = jnp.zeros((1, 512), F32)
    rows = lax.broadcasted_iota(jnp.int32, (BLOCK, 512), 0)

    def forward(sidx):
        for half in (0, 1):
            part = pl.ds(half * BLOCK, BLOCK)
            base = fold[2 * sidx + half] * BLOCK
            raw = nt(kv[sidx, 0, part, :], qs[...])
            ok = (rows >= first - base) & (rows <= pos - base)
            s2 = jnp.where(ok, raw * LOG2E, MASKED)
            sc[sidx, part, :] = s2
            gp = nt(kv[sidx, 1, part, :], dov[...])
            dp[sidx, part, :] = gp
            m = stat[0:1, :]
            m_new = jnp.maximum(m, jnp.max(s2, axis=0, keepdims=True))
            alpha = jnp.exp2(m - m_new)
            e = jnp.exp2(s2 - m_new)
            stat[0:1, :] = m_new
            stat[1:2, :] = stat[1:2, :] * alpha + jnp.sum(e, axis=0, keepdims=True)
            stat[2:3, :] = stat[2:3, :] * alpha + jnp.sum(e * gp, axis=0, keepdims=True)

    forward(s)
    va_p.wait_recv()
    v2a = same(vquarter(sid(-1, c), z, 0, 64), yp)
    vb_m.wait_recv()
    v2b = same(vquarter(sid(1, c), z, 64, 64), ym)
    vb_p.wait_recv()
    va_m.wait_recv()
    shares = {}
    for k in (-1, 1):
        shares[k] = (
            same(vquarter(sid(k, c), z, 0, 128), zp),
            same(vquarter(sid(k, c), z, 0, 128), zm),
        )
    own_pair.wait_recv()
    forward(sid(0, other))
    ka_p.wait_recv()
    k2a = same(kv.at[sid(-1, c), 0, pl.ds(0, 256)], yp)
    kb_m.wait_recv()
    k2b = same(kv.at[sid(1, c), 0, pl.ds(256, 256)], ym)

    def relay(k):
        shares[k][0].wait_recv()
        a = same(vquarter(sid(k, c), around(z, -1), 0, 64), zp)
        shares[k][1].wait_recv()
        b = same(vquarter(sid(k, c), around(z, 1), 64, 64), zm)
        return a, b

    v2a.wait_recv()
    v2b.wait_recv()
    shares[2] = (
        same(vquarter(sid(2, c), z, 0, 128), zp),
        same(vquarter(sid(2, c), z, 0, 128), zm),
    )
    relays = {-1: relay(-1), 1: relay(1)}
    kb_p.wait_recv()
    kpair = {-1: same(kv.at[sid(-1, c), 0], partner)}
    ka_m.wait_recv()
    kpair[1] = same(kv.at[sid(1, c), 0], partner)
    relays[2] = relay(2)
    vpair = {}
    for k in (-1, 1):
        for r in relays[k]:
            r.wait_recv()
        vpair[k] = same(kv.at[sid(k, c), 1], partner)
    for k in (-1, 1):
        forward(sid(k, c))
    for r in relays[2]:
        r.wait_recv()
    vpair[2] = same(kv.at[sid(2, c), 1], partner)
    k2a.wait_recv()
    k2b.wait_recv()
    kpair[2] = same(kv.at[sid(2, c), 0], partner)
    for k in (-1, 1):
        kpair[k].wait_recv()
        vpair[k].wait_recv()
        forward(sid(k, other))
    forward(sid(2, c))
    kpair[2].wait_recv()
    vpair[2].wait_recv()
    forward(sid(2, other))

    total = stat[1:2, :]
    lse = stat[0:1, :] + jnp.log2(total)
    gdot = stat[2:3, :] / total

    def backward(sidx, init=False):
        out = []
        for half in (0, 1):
            part = pl.ds(half * BLOCK, BLOCK)
            p = jnp.exp2(sc[sidx, part, :] - lse)
            ds = (p * (dp[sidx, part, :] - gdot)).astype(BF16)
            gv = nn(p.astype(BF16), dov[...])
            gk_ = nn(ds, qs[...])
            add = tn(kv[sidx, 0, part, :], ds)
            if init and half == 0:
                dqt[...] = add
            else:
                dqt[...] += add
            out.append((gk_, gv))
        return out

    def up(v):
        return v.astype(F32)

    offsets = (2, 1, -1, 0)
    pieces = [(xp, zi) for xp in range(4) for zi in range(4)]
    pairs, kc, vc = [], {}, {}

    def values_second(j):
        vc[j, 1].wait_recv()
        zi = around(z, 1)
        av[j, zi, 0:2] = (up(av[j, zi, 0:2]) + up(rv[0, j])).astype(BF16)
        vc[j, 4] = send(av.at[j, zi, pl.ds(0, 2)], fv.at[0, j, pl.ds(0, 2)], zp)
        vc[j, 2].wait_recv()
        zi = around(z, -1)
        av[j, zi, 2:4] = (up(av[j, zi, 2:4]) + up(rv[1, j])).astype(BF16)
        vc[j, 6] = send(av.at[j, zi, pl.ds(2, 2)], fv.at[1, j, pl.ds(2, 2)], zm)

    for j, k in enumerate(offsets):
        for half, (gk_, gv) in enumerate(backward(sid(k, other), j == 0)):
            psend[j, 0, pl.ds(half * BLOCK, BLOCK), :] = gk_.astype(BF16)
            psend[j, 1, pl.ds(half * BLOCK, BLOCK), :] = gv.astype(BF16)
        pairs.append(send(psend.at[j], precv.at[j], partner))
        mine = backward(sid(k, c))
        pairs[j].wait_recv()
        for half, (gk_, gv) in enumerate(mine):
            part = pl.ds(half * BLOCK, BLOCK)
            ak[j, part, :] = (gk_ + up(precv[j, 0, part, :])).astype(BF16)
            gv = (gv + up(precv[j, 1, part, :])).astype(BF16)
            for xp, zi in pieces:
                r0 = (4 * xp + zi) * 32 - half * BLOCK
                if 0 <= r0 < BLOCK:
                    av[j, zi, xp] = gv[r0 : r0 + 32, :]
        if j == 0:
            kc[1] = send(ak.at[0, pl.ds(0, 256)], rk.at[0], yp)
            kc[2] = send(ak.at[0, pl.ds(256, 256)], rk.at[1], ym)
        if j == 1:
            kc[3] = send(ak.at[1, pl.ds(256, 256)], fk.at[0, pl.ds(256, 256)], yp)
        if j == 2:
            kc[5] = send(ak.at[2, pl.ds(0, 256)], fk.at[1, pl.ds(0, 256)], ym)
        vc[j, 1] = send(av.at[j, around(z, 2), pl.ds(0, 2)], rv.at[0, j], zp)
        vc[j, 2] = send(av.at[j, around(z, 2), pl.ds(2, 2)], rv.at[1, j], zm)
        vc[j, 3] = send(av.at[j, around(z, 1), pl.ds(2, 2)], fv.at[0, j, pl.ds(2, 2)], zp)
        vc[j, 5] = send(av.at[j, around(z, -1), pl.ds(0, 2)], fv.at[1, j, pl.ds(0, 2)], zm)
        if j >= 2:
            values_second(j - 2)

    kc[1].wait_recv()
    ak[1, 0:256, :] = (up(ak[1, 0:256, :]) + up(rk[0])).astype(BF16)
    kc[4] = send(ak.at[1, pl.ds(0, 256)], fk.at[0, pl.ds(0, 256)], yp)
    kc[2].wait_recv()
    ak[2, 256:512, :] = (up(ak[2, 256:512, :]) + up(rk[1])).astype(BF16)
    kc[6] = send(ak.at[2, pl.ds(256, 256)], fk.at[1, pl.ds(256, 256)], ym)
    values_second(2)
    values_second(3)

    dqo[...] = (jnp.transpose(dqt[...]) * 0.0625).astype(BF16)
    dq_copy = pltpu.make_async_copy(dqo, dq_out.at[0], local_sem.at[0])
    dq_copy.start()

    def values_first_done(j):
        for i in (3, 4, 5, 6):
            vc[j, i].wait_recv()
        zv[j] = (up(av[j, z]) + up(fv[0, j]) + up(fv[1, j])).astype(BF16)

    ec = {}
    values_first_done(0)
    ec[1] = send(zv.at[0, pl.ds(0, 2)], ev.at[0], yp)
    ec[2] = send(zv.at[0, pl.ds(2, 2)], ev.at[1], ym)
    values_first_done(1)
    ec[3] = send(zv.at[1, pl.ds(2, 2)], fev.at[0, pl.ds(2, 2)], yp)
    values_first_done(2)
    ec[5] = send(zv.at[2, pl.ds(0, 2)], fev.at[1, pl.ds(0, 2)], ym)
    values_first_done(3)

    for i in (3, 4, 5, 6):
        kc[i].wait_recv()
    for xp, zi in pieces:
        r0 = (4 * xp + zi) * 32
        piece = pl.ds(r0, 32)
        yk[zi, xp] = (up(ak[3, piece, :]) + up(fk[0, piece, :]) + up(fk[1, piece, :])).astype(BF16)
    gc = {}
    zi2, zi1, zim = around(z, 2), around(z, 1), around(z, -1)
    gc[1] = send(yk.at[zi2, pl.ds(0, 2)], gk.at[0], zp)
    gc[2] = send(yk.at[zi2, pl.ds(2, 2)], gk.at[1], zm)
    gc[3] = send(yk.at[zi1, pl.ds(2, 2)], fgk.at[0, pl.ds(2, 2)], zp)
    gc[5] = send(yk.at[zim, pl.ds(0, 2)], fgk.at[1, pl.ds(0, 2)], zm)

    ec[1].wait_recv()
    zv[1, 0:2] = (up(zv[1, 0:2]) + up(ev[0])).astype(BF16)
    ec[4] = send(zv.at[1, pl.ds(0, 2)], fev.at[0, pl.ds(0, 2)], yp)
    ec[2].wait_recv()
    zv[2, 2:4] = (up(zv[2, 2:4]) + up(ev[1])).astype(BF16)
    ec[6] = send(zv.at[2, pl.ds(2, 2)], fev.at[1, pl.ds(2, 2)], ym)

    gc[1].wait_recv()
    yk[zi1, 0:2] = (up(yk[zi1, 0:2]) + up(gk[0])).astype(BF16)
    gc[4] = send(yk.at[zi1, pl.ds(0, 2)], fgk.at[0, pl.ds(0, 2)], zp)
    gc[2].wait_recv()
    yk[zim, 2:4] = (up(yk[zim, 2:4]) + up(gk[1])).astype(BF16)
    gc[6] = send(yk.at[zim, pl.ds(2, 2)], fgk.at[1, pl.ds(2, 2)], zm)

    for i in (3, 4, 5, 6):
        ec[i].wait_recv()
    gv = (up(zv[3]) + up(fev[0]) + up(fev[1])).astype(BF16)
    for xp in range(4):
        xs[xp, 1] = gv[xp]
    for i in (3, 4, 5, 6):
        gc[i].wait_recv()
    gk_ = (up(yk[z]) + up(fgk[0]) + up(fgk[1])).astype(BF16)
    for xp in range(4):
        xs[xp, 0] = gk_[xp]
    xc = []
    for k in (1, 2, 3):
        xc.append(send(xs.at[around(x, k)], rx.at[x], xo[k - 1]))
    rx[x] = xs[x]
    for cp in xc:
        cp.wait_recv()
    for r in (0, 1):
        dkv_out[0, r] = up(rx[2 * r, 0]) + up(rx[2 * r + 1, 0])
        dkv_out[1, r] = up(rx[2 * r, 1]) + up(rx[2 * r + 1, 1])
    outs = [
        pltpu.make_async_copy(dkv_out.at[0], dk_out, local_sem.at[1]),
        pltpu.make_async_copy(dkv_out.at[1], dv_out, local_sem.at[2]),
    ]
    for cp in outs:
        cp.start()
    for cp in started:
        cp.wait_send()
    dq_copy.wait()
    for cp in outs:
        cp.wait()


def per_device(queries, keys, values, d_out, doc_lengths, fold_order):
    hbm = pl.BlockSpec(memory_space=pl.ANY)
    smem = pl.BlockSpec(memory_space=pltpu.SMEM)

    def vm(*shape, dtype=BF16):
        return pltpu.VMEM(shape, dtype)

    return pl.pallas_call(
        kernel,
        out_shape=(
            jax.ShapeDtypeStruct((1, 512, 256), BF16),
            jax.ShapeDtypeStruct((2, 32, 256), F32),
            jax.ShapeDtypeStruct((2, 32, 256), F32),
        ),
        in_specs=[smem, smem, hbm, hbm, hbm, hbm],
        out_specs=(hbm, hbm, hbm),
        scratch_shapes=[
            vm(512, 256),
            vm(512, 256),
            vm(512, 256),
            vm(8, 2, 512, 256),
            vm(8, 512, 512, dtype=F32),
            vm(8, 512, 512, dtype=F32),
            vm(8, 512, dtype=F32),
            vm(256, 512, dtype=F32),
            vm(512, 256),
            vm(4, 2, 512, 256),
            vm(4, 2, 512, 256),
            vm(4, 512, 256),
            vm(4, 4, 4, 32, 256),
            vm(2, 256, 256),
            vm(2, 512, 256),
            vm(2, 4, 2, 32, 256),
            vm(2, 4, 4, 32, 256),
            vm(4, 4, 32, 256),
            vm(2, 2, 32, 256),
            vm(2, 4, 32, 256),
            vm(4, 4, 32, 256),
            vm(2, 2, 32, 256),
            vm(2, 4, 32, 256),
            vm(4, 2, 32, 256),
            vm(4, 2, 32, 256),
            vm(2, 2, 32, 256, dtype=F32),
            pltpu.SemaphoreType.DMA((4,)),
            pltpu.SemaphoreType.DMA((COPIES,)),
            pltpu.SemaphoreType.DMA((COPIES,)),
        ],
        compiler_params=pltpu.CompilerParams(
            collective_id=0, has_side_effects=True, vmem_limit_bytes=56 * 1024 * 1024
        ),
    )(doc_lengths, fold_order, queries, keys, values, d_out)


def solution(mesh):
    in_specs = (
        P("head", "seq", None),
        P(None, "seq", None),
        P(None, "seq", None),
        P("head", "seq", None),
        P(),
        P(),
    )
    out_specs = (
        P("head", "seq", None),
        P(None, ("seq", "head"), None),
        P(None, ("seq", "head"), None),
    )
    return jax.shard_map(
        per_device, mesh=mesh, in_specs=in_specs, out_specs=out_specs, check_vma=False
    )
```

time: 139 us -> 62.7 us (0.45)
  waiting for transfers between devices: 74 us -> 0 us
  Pallas kernels: 0 us -> 58.6 us
  matrix products: 26.1 us -> 0 us
  between operations: 14.2 us -> 0.65 us
  other arithmetic: 10.7 us -> 0 us
  starting transfers between devices: 6.94 us -> 0 us
  local copies, waits for them, and re-layouts: 6.96 us -> 3.2 us
    pallas_call x0 -> x1, Pallas kernels: none -> 58.6 us  [per_device(): pl.pallas_call(kernel, out_shape=(jax.ShapeDtypeStruct((1, 512, 256), BF1...]
    reduce_scatter x1 -> x0, waiting for transfers between devices: 38.1 us -> none  [side_by_side_2(): lax.psum_scatter(both, axis, scatter_dimension=dim, tiled=True)]
    all_gather x1 -> x0, waiting for transfers between devices: 30.6 us -> none  [side_by_side(): lax.all_gather(both, axis, axis=dim, tiled=True)]
    dot_general x6 -> x0, matrix products: 26.1 us -> none  [the longest x2 10.8 us: contract_last(): lax.dot_general(left, right, (((1,), (1,)), ((), ())), preferred_element_...]
    all_to_all x1 -> x0, starting transfers between devices: 6.86 us -> none  [sent_together(): lax.all_to_all(both, axis, split_axis=split_dim, concat_axis=concat_dim,...]
    reduce_sum x7 -> x0, other arithmetic: 6.44 us -> none  [the longest x1 3.39 us: per_device(): sum_next = jnp.sum(weights, axis=1, keepdims=True)]
    all_to_all x1 -> x0, waiting for transfers between devices: 5.22 us -> none  [sent_together(): lax.all_to_all(both, axis, split_axis=split_dim, concat_axis=concat_dim,...]
    concatenate x2 -> x0, other arithmetic: 3.31 us -> none  [the longest x1 2.47 us: side_by_side_2(): both = jnp.concatenate(arrays, axis=along)]
  transfers between devices with their start and end apart: 3 -> 0, of which waited for: 3 -> 0; matrix products, arithmetic and copies ran while one was open for 7% -> 0% of each run, Pallas kernels for 0% -> 0%
where the time goes in v1:
time: 62.7 us; the launch traced here: 62.5 us
  Pallas kernels  58.6 us (93%)
  local copies, waits for them, and re-layouts  3.2 us (5%)
  between operations  0.65 us (1%)
    pallas_call x1, Pallas kernels, per_device(): pl.pallas_call(kernel, out_shape=(jax.ShapeDtypeStruct((1, 512, 256), BF1...  58.6 us
    unnamed x7, local copies, waits for them, and re-layouts  3.2 us

profile of v1, /device:TPU:0, one launch (start us, length us, event | category | flops | bytes accessed | tf_op | source)
XLA Modules:
  0.0 62.5 jit_solution(3449108676937149018)
XLA Ops:
  0.6 58.6 %shard_map.85 = (bf16[1,512,256]{2,1,0:T(8,128)(2,1)}, f32[2,32,256]{2,1,0:T(8,128)}, f32[2,32,256]{2,1,0:T(8,128)}) custom-call(s32[2,8]{1,0:T(2,128)} %lengths.1, s32[16]{0:T(128)} %fold.1, bf16[1,512,256]{2,1,0:T(8,128)(2,1)} %q_hbm.1, bf16[2,512,256]{2,1,0:T(8,128)(2,1)} %k_hbm.1, bf16[2,512,256]{2,1,0:T(8,128)(2,1)} %v_hbm.1, bf16[1,512,256]{2,1,0:T(8,128)(2,1)} %do_hbm.1), custom_call_target="tpu_custom_call" | custom-call | tf_op jit(solution)/shard_map/pallas_call | solution.py:360
  59.3 0.0 copy-start.1
  59.3 1.7 %copy.12 = bf16[1,512,256]{2,1,0:T(8,128)(2,1)} copy(bf16[1,512,256]{2,1,0:T(8,128)(2,1)} %get-tuple-element.6) | data formatting | bytes 524288
  61.0 0.0 copy-done.1
  61.0 0.0 copy-start
  61.0 0.6 %copy.13 = f32[2,32,256]{2,1,0:T(8,128)} copy(f32[2,32,256]{2,1,0:T(8,128)S(1)} %copy-done.1) | data formatting | bytes 131072
  61.6 0.2 copy-done
  61.9 0.6 %copy.14 = f32[2,32,256]{2,1,0:T(8,128)} copy(f32[2,32,256]{2,1,0:T(8,128)S(1)} %copy-done) | data formatting | bytes 131072
Async XLA Ops:
  59.3 1.7 %copy-start.1 = (f32[2,32,256]{2,1,0:T(8,128)S(1)}, f32[2,32,256]{2,1,0:T(8,128)}, u32[]{:S(2)}) copy-start(f32[2,32,256]{2,1,0:T(8,128)} %get-tuple-element.7) | copy-start | bytes 196612
  61.0 0.9 %copy-start = (f32[2,32,256]{2,1,0:T(8,128)S(1)}, f32[2,32,256]{2,1,0:T(8,128)}, u32[]{:S(2)}) copy-start(f32[2,32,256]{2,1,0:T(8,128)} %get-tuple-element.8) | copy-start | bytes 196612

commit v2 on v1

--- a/solution.py
+++ b/solution.py
@@ -30,8 +30,8 @@
 def kernel(
     lengths, fold, q_hbm, k_hbm, v_hbm, do_hbm,
     dq_out, dk_out, dv_out,
-    qv, dov, qs, kv, sc, dp, stat, dqt, dqo,
-    psend, precv, ak, av, rk, fk, rv, fv, zv, ev, fev, yk, gk, fgk, xs, rx, dkv_out,
+    qv, dov, qs, kv, sc, dp, stat, dsb, dqt,
+    psend, precv, ak, av, rk, fk, rv, fv, zv, ev, fev, yk, gk, fgk, xs, rx,
     local_sem, send_sem, recv_sem,
 ):
     s = lax.axis_index("seq")
@@ -97,8 +97,6 @@
     loads[1].wait()
     ka_p = same(kv.at[s, 0, pl.ds(0, 256)], yp)
     kb_m = same(kv.at[s, 0, pl.ds(256, 256)], ym)
-    kb_p = same(kv.at[s, 0, pl.ds(256, 256)], yp)
-    ka_m = same(kv.at[s, 0, pl.ds(0, 256)], ym)
     own_pair = same(kv.at[s], partner)
 
     lane = lax.broadcasted_iota(jnp.int32, (1, 512), 1)
@@ -141,6 +139,8 @@
     v2a = same(vquarter(sid(-1, c), z, 0, 64), yp)
     vb_m.wait_recv()
     v2b = same(vquarter(sid(1, c), z, 64, 64), ym)
+    kb_p = same(kv.at[s, 0, pl.ds(256, 256)], yp)
+    ka_m = same(kv.at[s, 0, pl.ds(0, 256)], ym)
     vb_p.wait_recv()
     va_m.wait_recv()
     shares = {}
@@ -201,21 +201,21 @@
     lse = stat[0:1, :] + jnp.log2(total)
     gdot = stat[2:3, :] / total
 
-    def backward(sidx, init=False):
+    def backward(sidx):
         out = []
         for half in (0, 1):
             part = pl.ds(half * BLOCK, BLOCK)
             p = jnp.exp2(sc[sidx, part, :] - lse)
             ds = (p * (dp[sidx, part, :] - gdot)).astype(BF16)
-            gv = nn(p.astype(BF16), dov[...])
-            gk_ = nn(ds, qs[...])
-            add = tn(kv[sidx, 0, part, :], ds)
-            if init and half == 0:
-                dqt[...] = add
-            else:
-                dqt[...] += add
-            out.append((gk_, gv))
+            dsb[sidx, part, :] = ds
+            out.append((nn(ds, qs[...]), nn(p.astype(BF16), dov[...])))
         return out
+
+    def queries(sidxs):
+        total = tn(kv[sidxs[0], 0], dsb[sidxs[0]])
+        for sidx in sidxs[1:]:
+            total = total + tn(kv[sidx, 0], dsb[sidx])
+        return total
 
     def up(v):
         return v.astype(F32)
@@ -234,12 +234,14 @@
         av[j, zi, 2:4] = (up(av[j, zi, 2:4]) + up(rv[1, j])).astype(BF16)
         vc[j, 6] = send(av.at[j, zi, pl.ds(2, 2)], fv.at[1, j, pl.ds(2, 2)], zm)
 
-    for j, k in enumerate(offsets):
-        for half, (gk_, gv) in enumerate(backward(sid(k, other), j == 0)):
+    def theirs(j):
+        for half, (gk_, gv) in enumerate(backward(sid(offsets[j], other))):
             psend[j, 0, pl.ds(half * BLOCK, BLOCK), :] = gk_.astype(BF16)
             psend[j, 1, pl.ds(half * BLOCK, BLOCK), :] = gv.astype(BF16)
         pairs.append(send(psend.at[j], precv.at[j], partner))
-        mine = backward(sid(k, c))
+
+    def ours(j):
+        mine = backward(sid(offsets[j], c))
         pairs[j].wait_recv()
         for half, (gk_, gv) in enumerate(mine):
             part = pl.ds(half * BLOCK, BLOCK)
@@ -260,9 +262,17 @@
         vc[j, 2] = send(av.at[j, around(z, 2), pl.ds(2, 2)], rv.at[1, j], zm)
         vc[j, 3] = send(av.at[j, around(z, 1), pl.ds(2, 2)], fv.at[0, j, pl.ds(2, 2)], zp)
         vc[j, 5] = send(av.at[j, around(z, -1), pl.ds(0, 2)], fv.at[1, j, pl.ds(0, 2)], zm)
-        if j >= 2:
-            values_second(j - 2)
-
+
+    theirs(0)
+    theirs(1)
+    ours(0)
+    theirs(2)
+    ours(1)
+    theirs(3)
+    ours(2)
+    values_second(0)
+    ours(3)
+    values_second(1)
     kc[1].wait_recv()
     ak[1, 0:256, :] = (up(ak[1, 0:256, :]) + up(rk[0])).astype(BF16)
     kc[4] = send(ak.at[1, pl.ds(0, 256)], fk.at[0, pl.ds(0, 256)], yp)
@@ -272,9 +282,7 @@
     values_second(2)
     values_second(3)
 
-    dqo[...] = (jnp.transpose(dqt[...]) * 0.0625).astype(BF16)
-    dq_copy = pltpu.make_async_copy(dqo, dq_out.at[0], local_sem.at[0])
-    dq_copy.start()
+    dqt[...] = queries((0, 1, 2, 3))
 
     def values_first_done(j):
         for i in (3, 4, 5, 6):
@@ -304,6 +312,7 @@
     gc[3] = send(yk.at[zi1, pl.ds(2, 2)], fgk.at[0, pl.ds(2, 2)], zp)
     gc[5] = send(yk.at[zim, pl.ds(0, 2)], fgk.at[1, pl.ds(0, 2)], zm)
 
+    dq_out[0] = (jnp.transpose(dqt[...] + queries((4, 5, 6, 7))) * 0.0625).astype(BF16)
     ec[1].wait_recv()
     zv[1, 0:2] = (up(zv[1, 0:2]) + up(ev[0])).astype(BF16)
     ec[4] = send(zv.at[1, pl.ds(0, 2)], fev.at[0, pl.ds(0, 2)], yp)
@@ -335,37 +344,37 @@
     for cp in xc:
         cp.wait_recv()
     for r in (0, 1):
-        dkv_out[0, r] = up(rx[2 * r, 0]) + up(rx[2 * r + 1, 0])
-        dkv_out[1, r] = up(rx[2 * r, 1]) + up(rx[2 * r + 1, 1])
-    outs = [
-        pltpu.make_async_copy(dkv_out.at[0], dk_out, local_sem.at[1]),
-        pltpu.make_async_copy(dkv_out.at[1], dv_out, local_sem.at[2]),
-    ]
-    for cp in outs:
-        cp.start()
+        dk_out[r] = up(rx[2 * r, 0]) + up(rx[2 * r + 1, 0])
+        dv_out[r] = up(rx[2 * r, 1]) + up(rx[2 * r + 1, 1])
     for cp in started:
         cp.wait_send()
-    dq_copy.wait()
-    for cp in outs:
+
+
+def leave(a, b, c, a_out, b_out, c_out, sem):
+    moves = [pltpu.make_async_copy(src, dst, sem.at[i]) for i, (src, dst) in enumerate(((a, a_out), (b, b_out), (c, c_out)))]
+    for cp in moves:
+        cp.start()
+    for cp in moves:
         cp.wait()
 
 
 def per_device(queries, keys, values, d_out, doc_lengths, fold_order):
     hbm = pl.BlockSpec(memory_space=pl.ANY)
+    vmem = pl.BlockSpec(memory_space=pltpu.VMEM)
     smem = pl.BlockSpec(memory_space=pltpu.SMEM)
 
     def vm(*shape, dtype=BF16):
         return pltpu.VMEM(shape, dtype)
 
-    return pl.pallas_call(
+    grads = pl.pallas_call(
         kernel,
         out_shape=(
-            jax.ShapeDtypeStruct((1, 512, 256), BF16),
-            jax.ShapeDtypeStruct((2, 32, 256), F32),
-            jax.ShapeDtypeStruct((2, 32, 256), F32),
+            pltpu.VMEM((1, 512, 256), BF16),
+            pltpu.VMEM((2, 32, 256), F32),
+            pltpu.VMEM((2, 32, 256), F32),
         ),
         in_specs=[smem, smem, hbm, hbm, hbm, hbm],
-        out_specs=(hbm, hbm, hbm),
+        out_specs=(vmem, vmem, vmem),
         scratch_shapes=[
             vm(512, 256),
             vm(512, 256),
@@ -374,8 +383,8 @@
             vm(8, 512, 512, dtype=F32),
             vm(8, 512, 512, dtype=F32),
             vm(8, 512, dtype=F32),
+            vm(8, 512, 512),
             vm(256, 512, dtype=F32),
-            vm(512, 256),
             vm(4, 2, 512, 256),
             vm(4, 2, 512, 256),
             vm(4, 512, 256),
@@ -392,15 +401,22 @@
             vm(2, 4, 32, 256),
             vm(4, 2, 32, 256),
             vm(4, 2, 32, 256),
-            vm(2, 2, 32, 256, dtype=F32),
             pltpu.SemaphoreType.DMA((4,)),
             pltpu.SemaphoreType.DMA((COPIES,)),
             pltpu.SemaphoreType.DMA((COPIES,)),
         ],
         compiler_params=pltpu.CompilerParams(
-            collective_id=0, has_side_effects=True, vmem_limit_bytes=56 * 1024 * 1024
+            collective_id=0, has_side_effects=True, vmem_limit_bytes=66600000
         ),
     )(doc_lengths, fold_order, queries, keys, values, d_out)
+    return pl.pallas_call(
+        leave,
+        out_shape=tuple(jax.ShapeDtypeStruct(g.shape, g.dtype) for g in grads),
+        in_specs=[vmem] * 3,
+        out_specs=(hbm,) * 3,
+        scratch_shapes=[pltpu.SemaphoreType.DMA((3,))],
+        compiler_params=pltpu.CompilerParams(vmem_limit_bytes=1024 * 1024),
+    )(*grads)
 
 
 def solution(mesh):

time: 62.7 us -> 54 us (0.86)
  Pallas kernels: 58.6 us -> 52.9 us
  local copies, waits for them, and re-layouts: 3.2 us -> 0 us
    pallas_call x1 -> x2, Pallas kernels: 58.6 us -> 52.9 us  [the longest x1 52.2 us: per_device(): pl.pallas_call(kernel, out_shape=(pltpu.VMEM((1, 512, 256), BF16), pltpu....]
    unnamed x7 -> x0, local copies, waits for them, and re-layouts: 3.2 us -> none
where the time goes in v2:
time: 54 us; the launch traced here: 53.6 us
  Pallas kernels  52.9 us (98%)
  between operations  0.64 us (1%)
    pallas_call x1, Pallas kernels, per_device(): pl.pallas_call(kernel, out_shape=(pltpu.VMEM((1, 512, 256), BF16), pltpu....  52.2 us

profile of v2, /device:TPU:0, one launch (start us, length us, event | category | flops | bytes accessed | tf_op | source)
XLA Modules:
  0.0 53.6 jit_solution(7503999298735635126)
XLA Ops:
  0.6 52.2 %shard_map.85 = (bf16[1,512,256]{2,1,0:T(8,128)(2,1)S(1)}, f32[2,32,256]{2,1,0:T(8,128)S(1)}, f32[2,32,256]{2,1,0:T(8,128)S(1)}) custom-call(s32[2,8]{1,0:T(2,128)} %lengths.1, s32[16]{0:T(128)} %fold.1, bf16[1,512,256]{2,1,0:T(8,128)(2,1)} %q_hbm.1, bf16[2,512,256]{2,1,0:T(8,128)(2,1)} %k_hbm.1, bf16[2,512,256]{2,1,0:T(8,128)(2,1)} %v_hbm.1, ...), custom_call_target="tpu_custom_call" | custom-call | tf_op jit(solution)/shard_map/pallas_call | solution.py:369
  52.8 0.8 %shard_map.86 = (bf16[1,512,256]{2,1,0:T(8,128)(2,1)}, f32[2,32,256]{2,1,0:T(8,128)}, f32[2,32,256]{2,1,0:T(8,128)}) custom-call(bf16[1,512,256]{2,1,0:T(8,128)(2,1)S(1)} %get-tuple-element.6.a, f32[2,32,256]{2,1,0:T(8,128)S(1)} %get-tuple-element.7.b, f32[2,32,256]{2,1,0:T(8,128)S(1)} %get-tuple-element.8.c), custom_call_target="tpu_custom_call" | custom-call | tf_op jit(solution)/shard_map/pallas_call | solution.py:412

commit v3 on v2

v3 whole, which is shorter than its diff:
```python
import jax
import jax.numpy as jnp
from jax import lax
from jax.experimental import pallas as pl
from jax.experimental.pallas import tpu as pltpu
from jax.sharding import PartitionSpec as P

MESH = pl.DeviceIdType.MESH
LOG2E = 1.4426950408889634
MASKED = -1e30
BLOCK = 256
F32 = jnp.float32
BF16 = jnp.bfloat16
ROW_HEADS = 8
COPIES = 112
LOW = 256


def nt(a, b):
    return lax.dot_general(a, b, (((1,), (1,)), ((), ())), preferred_element_type=F32)


def nn(a, b):
    return lax.dot_general(a, b, (((1,), (0,)), ((), ())), preferred_element_type=F32)


def tn(a, b):
    return lax.dot_general(a, b, (((0,), (0,)), ((), ())), preferred_element_type=F32)


def kernel(
    lengths, fold, q_hbm, k_hbm, v_hbm, do_hbm,
    dq_out, dk_out, dv_out,
    qv, dov, qs, qst, dot_, kv, sc, dp, stat, stat2, dsb, dqt, dqs, dqr,
    ak, av, rk, fk, dk2, rv, fv, dv2, zv, fev, yk, fgk, xs, rx,
    local_sem, send_sem, recv_sem,
):
    s = lax.axis_index("seq")
    h = lax.axis_index("head")
    y, c = lax.div(s, 2), lax.rem(s, 2)
    x, z = lax.div(h, 4), lax.rem(h, 4)
    row = lax.div(h, ROW_HEADS)

    def around(v, k):
        return lax.rem(v + (k % 4), 4)

    partner = {"seq": 2 * y + (1 - c), "head": h}
    yp = {"seq": 2 * around(y, 1) + c, "head": h}
    ym = {"seq": 2 * around(y, -1) + c, "head": h}
    yf = {"seq": 2 * around(y, 2) + c, "head": h}
    zp = {"seq": s, "head": 4 * x + around(z, 1)}
    zm = {"seq": s, "head": 4 * x + around(z, -1)}
    diag = {
        (i, j): {"seq": 2 * around(y, i) + c, "head": 4 * x + around(z, j)} for i in (-1, 1) for j in (-1, 1)
    }
    xo = [{"seq": s, "head": 4 * around(x, k) + z} for k in (1, 2, 3)]

    mine = pl.ds(pl.multiple_of(512 * c, 512), 512)
    theirs = pl.ds(pl.multiple_of(512 * (1 - c), 512), 512)

    loads = [
        pltpu.make_async_copy(v_hbm.at[row], kv.at[y, 1], local_sem.at[0]),
        pltpu.make_async_copy(k_hbm.at[row], kv.at[y, 0], local_sem.at[1]),
        pltpu.make_async_copy(q_hbm.at[0], qv.at[mine], local_sem.at[2]),
        pltpu.make_async_copy(do_hbm.at[0], dov.at[mine], local_sem.at[3]),
    ]
    for cp in loads:
        cp.start()

    barrier = pltpu.get_barrier_semaphore()
    peers = [partner, yp, ym, yf, zp, zm] + list(diag.values()) + xo
    for peer in peers:
        pl.semaphore_signal(barrier, inc=1, device_id=peer, device_id_type=MESH)
    pl.semaphore_wait(barrier, len(peers))

    started = []

    def send(src, dst, device):
        i = len(started)
        cp = pltpu.make_async_remote_copy(
            src_ref=src, dst_ref=dst, send_sem=send_sem.at[i], recv_sem=recv_sem.at[i],
            device_id=device, device_id_type=MESH,
        )
        cp.start()
        started.append(cp)
        return cp

    def same(ref, device):
        return send(ref, ref, device)

    def chip(k):
        return around(y, k)

    zq = 128 * z

    def vquarter(yi, zi, lo, n):
        return kv.at[yi, 1, pl.ds(pl.multiple_of(128 * zi + lo, 64), n)]

    low, high = pl.ds(0, LOW), pl.ds(LOW, 512 - LOW)
    loads[0].wait()
    v_p = same(vquarter(y, z, 0, 128), yp)
    v_m = same(vquarter(y, z, 0, 128), ym)
    v_f = same(vquarter(y, z, 0, 128), yf)
    loads[1].wait()
    ka_p = same(kv.at[y, 0, low], yp)
    kb_m = same(kv.at[y, 0, high], ym)
    loads[2].wait()
    q_pair = same(qv.at[mine], partner)
    loads[3].wait()
    do_pair = same(dov.at[mine], partner)

    lane = lax.broadcasted_iota(jnp.int32, (1, 1024), 1)
    pos = lane + fold[4 * y] * BLOCK
    for b in (1, 2, 3):
        pos = jnp.where(lane < BLOCK * b, pos, lane + (fold[4 * y + b] - b) * BLOCK)
    first = jnp.zeros((1, 1024), jnp.int32)
    at = jnp.int32(0)
    for d in range(8):
        first = jnp.where(pos >= at, at, first)
        at = at + lengths[row, d]
    rows = lax.broadcasted_iota(jnp.int32, (BLOCK, 1024), 0)
    stat[0:1, :] = jnp.full((1, 1024), MASKED, F32)
    stat[1:3, :] = jnp.zeros((2, 1024), F32)
    stat[3:4, :] = jnp.full((1, 1024), MASKED, F32)
    stat[4:8, :] = jnp.zeros((4, 1024), F32)
    q_pair.wait_recv()
    qs[...] = (qv[...].astype(F32) * 0.0625).astype(BF16)
    qst[...] = jnp.transpose(qs[...])
    do_pair.wait_recv()
    dot_[...] = jnp.transpose(dov[...])

    offsets = (2, 1, -1, 0)

    parts = [pl.ds(half * BLOCK, BLOCK) for half in (0, 1)]

    def scores(j):
        yi = chip(offsets[j])
        m = stat[0:1, :]
        for half, part in enumerate(parts):
            base = fold[4 * yi + 2 * c + half] * BLOCK
            raw = nn(kv[yi, 0, part, :], qst[...])
            ok = (rows >= first - base) & (rows <= pos - base)
            s2 = jnp.where(ok, raw * LOG2E, MASKED)
            sc[j, part, :] = s2
            m = jnp.maximum(m, jnp.max(s2, axis=0, keepdims=True))
        stat[0:1, :] = m

    def probs(j):
        yi = chip(offsets[j])
        m = stat[0:1, :]
        alpha = jnp.exp2(stat[3:4, :] - m)
        total = stat[1:2, :] * alpha
        dot = stat[2:3, :] * alpha
        for part in parts:
            gp = nn(kv[yi, 1, part, :], dot_[...])
            dp[j, part, :] = gp
            e = jnp.exp2(sc[j, part, :] - m)
            total = total + jnp.sum(e, axis=0, keepdims=True)
            dot = dot + jnp.sum(e * gp, axis=0, keepdims=True)
        stat[1:2, :] = total
        stat[2:3, :] = dot
        stat[3:4, :] = m

    shares, relays = {}, {}

    def share(k):
        shares[k] = (
            same(vquarter(chip(k), z, 0, 128), zp),
            same(vquarter(chip(k), z, 0, 128), zm),
        )

    def relay(k):
        shares[k][0].wait_recv()
        a = same(vquarter(chip(k), around(z, -1), 0, 64), zp)
        shares[k][1].wait_recv()
        relays[k] = a, same(vquarter(chip(k), around(z, 1), 64, 64), zm)

    v_p.wait_recv()
    share(-1)
    v_m.wait_recv()
    share(1)
    kb_p = same(kv.at[y, 0, high], yp)
    ka_m = same(kv.at[y, 0, low], ym)
    v_f.wait_recv()
    share(2)
    ka_p.wait_recv()
    k2a = same(kv.at[chip(-1), 0, low], yp)
    kb_m.wait_recv()
    k2b = same(kv.at[chip(1), 0, high], ym)
    scores(3)
    probs(3)
    relay(-1)
    relay(1)
    kb_p.wait_recv()
    ka_m.wait_recv()
    scores(1)
    relay(2)
    scores(2)
    for k in (-1, 1):
        for r in relays[k]:
            r.wait_recv()
    probs(1)
    probs(2)
    k2a.wait_recv()
    k2b.wait_recv()
    scores(0)
    for r in relays[2]:
        r.wait_recv()
    probs(0)

    stat_pair = send(stat, stat2, partner)
    stat_pair.wait_recv()
    top = jnp.maximum(stat[0:1, :], stat2[0:1, :])
    w1 = jnp.exp2(stat[0:1, :] - top)
    w2 = jnp.exp2(stat2[0:1, :] - top)
    total = stat[1:2, :] * w1 + stat2[1:2, :] * w2
    lse = top + jnp.log2(total)
    gdot = (stat[2:3, :] * w1 + stat2[2:3, :] * w2) / total

    def backward(j):
        out = []
        for half in (0, 1):
            part = pl.ds(half * BLOCK, BLOCK)
            p = jnp.exp2(sc[j, part, :] - lse)
            ds = (p * (dp[j, part, :] - gdot)).astype(BF16)
            dsb[j, part, :] = ds
            out.append((nn(ds, qs[...]), nn(p.astype(BF16), dov[...])))
        return out

    def queries():
        acc = tn(kv[chip(offsets[0]), 0], dsb[0])
        for j in (1, 2, 3):
            acc = acc + tn(kv[chip(offsets[j]), 0], dsb[j])
        return acc

    def up(v):
        return v.astype(F32)

    pieces = [(xp, zi) for xp in range(4) for zi in range(4)]
    place = [lax.rem(zi - z + 5, 4) for zi in range(4)]
    lo, hi = pl.ds(0, 2), pl.ds(2, 2)
    near, far = pl.ds(0, 3), 3
    kc, vc = {}, {}

    def values_second(j):
        vc[j, 1].wait_recv()
        av[j, 2, 0:2] = (up(av[j, 2, 0:2]) + up(rv[0, j])).astype(BF16)
        if j == 0:
            vc[j, 4] = send(av.at[j, 2, lo], dv2.at[0, 0], diag[1, 1])
        else:
            vc[j, 4] = send(av.at[j, 2, lo], fv.at[0, j, lo], zp)
        vc[j, 2].wait_recv()
        av[j, 0, 2:4] = (up(av[j, 0, 2:4]) + up(rv[1, j])).astype(BF16)
        if j == 0:
            vc[j, 6] = send(av.at[j, 0, hi], dv2.at[1, 0], diag[-1, -1])
        else:
            vc[j, 6] = send(av.at[j, 0, hi], fv.at[1, j, hi], zm)

    def values_early():
        vc[0, 5].wait_recv()
        av[0, 1, 0:2] = (up(av[0, 1, 0:2]) + up(fv[1, 0, 0:2])).astype(BF16)
        vc[0, 7] = send(av.at[0, 1, lo], dv2.at[0, 1], yp)
        vc[0, 3].wait_recv()
        av[0, 1, 2:4] = (up(av[0, 1, 2:4]) + up(fv[0, 0, 2:4])).astype(BF16)
        vc[0, 8] = send(av.at[0, 1, hi], dv2.at[1, 1], ym)

    def keys_early():
        kc[5].wait_recv()
        ak[3, 3, 0:2] = (up(ak[3, 3, 0:2]) + up(fk[1, 3, 0:2])).astype(BF16)
        kc[17] = send(ak.at[3, far, lo], dk2.at[0, 1], zp)
        kc[3].wait_recv()
        ak[3, 3, 2:4] = (up(ak[3, 3, 2:4]) + up(fk[0, 3, 2:4])).astype(BF16)
        kc[18] = send(ak.at[3, far, hi], dk2.at[1, 1], zm)

    def block(j):
        for half, (gk_, gv) in enumerate(backward(j)):
            gk_, gv = gk_.astype(BF16), gv.astype(BF16)
            for xp, zi in pieces:
                r0 = (4 * xp + zi) * 32 - half * BLOCK
                if 0 <= r0 < BLOCK:
                    ak[j, place[zi], xp] = gk_[r0 : r0 + 32, :]
                    av[j, place[zi], xp] = gv[r0 : r0 + 32, :]
        for half in (0, 1):
            at_ = (lo, hi)[half]
            to = (zp, zm)[half]
            vc[j, 1 + half] = send(av.at[j, far, at_], rv.at[half, j], to)
            if j == 0:
                kc[1 + half] = send(ak.at[0, pl.ds(0, 4), at_], rk.at[half], (yp, ym)[half])
            if j == 1 and half == 1:
                kc[3] = send(ak.at[1, pl.ds(0, 4), hi], fk.at[0, pl.ds(0, 4), hi], yp)
            if j == 2 and half == 0:
                kc[5] = send(ak.at[2, pl.ds(0, 4), lo], fk.at[1, pl.ds(0, 4), lo], ym)
            if half == 0:
                vc[j, 5] = send(av.at[j, 0, lo], fv.at[1, j, lo], zm)
            else:
                vc[j, 3] = send(av.at[j, 2, hi], fv.at[0, j, hi], zp)

    block(0)
    block(1)
    block(2)
    values_second(0)
    block(3)
    values_early()
    values_second(1)
    kc[1].wait_recv()
    ak[1, :, 0:2] = (up(ak[1, :, 0:2]) + up(rk[0])).astype(BF16)
    kc[14] = send(ak.at[1, far, lo], dk2.at[0, 0], diag[1, 1])
    kc[4] = send(ak.at[1, near, lo], fk.at[0, pl.ds(0, 3), lo], yp)
    kc[2].wait_recv()
    ak[2, :, 2:4] = (up(ak[2, :, 2:4]) + up(rk[1])).astype(BF16)
    kc[16] = send(ak.at[2, far, hi], dk2.at[1, 0], diag[-1, -1])
    kc[6] = send(ak.at[2, near, hi], fk.at[1, pl.ds(0, 3), hi], ym)
    values_second(2)
    values_second(3)

    keys_early()
    dqt[...] = queries()
    dqs[...] = jnp.transpose(dqt[:, theirs])
    dq_pair = send(dqs, dqr, partner)

    def values_along_z(j):
        for i in (3, 4, 5, 6):
            vc[j, i].wait_recv()
        return up(av[j, 1]) + up(fv[0, j]) + up(fv[1, j])

    for i in (4, 6, 7, 8):
        vc[0, i].wait_recv()
    ec = {}
    w = values_along_z(1)
    zv[0, 0:2] = (w[0:2] + up(dv2[0, 0]) + up(dv2[0, 1])).astype(BF16)
    zv[0, 2:4] = w[2:4].astype(BF16)
    ec[0] = send(zv.at[0], fev.at[0], yp)
    w = values_along_z(2)
    zv[1, 0:2] = w[0:2].astype(BF16)
    zv[1, 2:4] = (w[2:4] + up(dv2[1, 0]) + up(dv2[1, 1])).astype(BF16)
    ec[1] = send(zv.at[1], fev.at[1], ym)

    for i in (4, 6):
        kc[i].wait_recv()

    def keys_along_y(q):
        return up(ak[3, q]) + up(fk[0, q]) + up(fk[1, q])

    for i in (14, 16, 17, 18):
        kc[i].wait_recv()
    gc = {}
    w = keys_along_y(2)
    yk[0, 0:2] = (w[0:2] + up(dk2[0, 0]) + up(dk2[0, 1])).astype(BF16)
    yk[0, 2:4] = w[2:4].astype(BF16)
    gc[0] = send(yk.at[0], fgk.at[0], zp)
    w = keys_along_y(0)
    yk[1, 0:2] = w[0:2].astype(BF16)
    yk[1, 2:4] = (w[2:4] + up(dk2[1, 0]) + up(dk2[1, 1])).astype(BF16)
    gc[1] = send(yk.at[1], fgk.at[1], zm)

    w = values_along_z(3)
    for cp in ec.values():
        cp.wait_recv()
    xs[1] = (w + up(fev[0]) + up(fev[1])).astype(BF16)
    xc = []
    for k in (1, 2, 3):
        xc.append(send(xs.at[1, around(x, k)], rx.at[1, x], xo[k - 1]))
    dq_pair.wait_recv()
    dq_out[0] = ((jnp.transpose(dqt[:, mine]) + dqr[...]) * 0.0625).astype(BF16)
    for cp in gc.values():
        cp.wait_recv()
    xs[0] = (keys_along_y(1) + up(fgk[0]) + up(fgk[1])).astype(BF16)
    for k in (1, 2, 3):
        xc.append(send(xs.at[0, around(x, k)], rx.at[0, x], xo[k - 1]))
    rx[0, x] = xs[0, x]
    rx[1, x] = xs[1, x]
    for cp in xc:
        cp.wait_recv()
    for r in (0, 1):
        dk_out[r] = up(rx[0, 2 * r]) + up(rx[0, 2 * r + 1])
        dv_out[r] = up(rx[1, 2 * r]) + up(rx[1, 2 * r + 1])
    for cp in started:
        cp.wait_send()


def leave(a, b, c, a_out, b_out, c_out, sem):
    moves = [pltpu.make_async_copy(src, dst, sem.at[i]) for i, (src, dst) in enumerate(((a, a_out), (b, b_out), (c, c_out)))]
    for cp in moves:
        cp.start()
    for cp in moves:
        cp.wait()


def per_device(queries, keys, values, d_out, doc_lengths, fold_order):
    hbm = pl.BlockSpec(memory_space=pl.ANY)
    vmem = pl.BlockSpec(memory_space=pltpu.VMEM)
    smem = pl.BlockSpec(memory_space=pltpu.SMEM)

    def vm(*shape, dtype=BF16):
        return pltpu.VMEM(shape, dtype)

    grads = pl.pallas_call(
        kernel,
        out_shape=(
            pltpu.VMEM((1, 512, 256), BF16),
            pltpu.VMEM((2, 32, 256), F32),
            pltpu.VMEM((2, 32, 256), F32),
        ),
        in_specs=[smem, smem, hbm, hbm, hbm, hbm],
        out_specs=(vmem, vmem, vmem),
        scratch_shapes=[
            vm(1024, 256),
            vm(1024, 256),
            vm(1024, 256),
            vm(256, 1024),
            vm(256, 1024),
            vm(4, 2, 512, 256),
            vm(4, 512, 1024, dtype=F32),
            vm(4, 512, 1024, dtype=F32),
            vm(8, 1024, dtype=F32),
            vm(8, 1024, dtype=F32),
            vm(4, 512, 1024),
            vm(256, 1024, dtype=F32),
            vm(512, 256, dtype=F32),
            vm(512, 256, dtype=F32),
            vm(4, 4, 4, 32, 256),
            vm(4, 4, 4, 32, 256),
            vm(2, 4, 2, 32, 256),
            vm(2, 4, 4, 32, 256),
            vm(2, 2, 2, 32, 256),
            vm(2, 4, 2, 32, 256),
            vm(2, 4, 4, 32, 256),
            vm(2, 2, 2, 32, 256),
            vm(2, 4, 32, 256),
            vm(2, 4, 32, 256),
            vm(2, 4, 32, 256),
            vm(2, 4, 32, 256),
            vm(2, 4, 32, 256),
            vm(2, 4, 32, 256),
            pltpu.SemaphoreType.DMA((4,)),
            pltpu.SemaphoreType.DMA((COPIES,)),
            pltpu.SemaphoreType.DMA((COPIES,)),
        ],
        compiler_params=pltpu.CompilerParams(
            collective_id=0, has_side_effects=True, vmem_limit_bytes=66600000
        ),
    )(doc_lengths, fold_order, queries, keys, values, d_out)
    return pl.pallas_call(
        leave,
        out_shape=tuple(jax.ShapeDtypeStruct(g.shape, g.dtype) for g in grads),
        in_specs=[vmem] * 3,
        out_specs=(hbm,) * 3,
        scratch_shapes=[pltpu.SemaphoreType.DMA((3,))],
        compiler_params=pltpu.CompilerParams(vmem_limit_bytes=1024 * 1024),
    )(*grads)


def solution(mesh):
    in_specs = (
        P("head", "seq", None),
        P(None, "seq", None),
        P(None, "seq", None),
        P("head", "seq", None),
        P(),
        P(),
    )
    out_specs = (
        P("head", "seq", None),
        P(None, ("seq", "head"), None),
        P(None, ("seq", "head"), None),
    )
    return jax.shard_map(
        per_device, mesh=mesh, in_specs=in_specs, out_specs=out_specs, check_vma=False
    )
```

time: 54 us -> 49.4 us (0.915)
  Pallas kernels: 52.9 us -> 48.6 us
    pallas_call x1, Pallas kernels: 52.2 us -> 47.9 us  [per_device(): pl.pallas_call(kernel, out_shape=(pltpu.VMEM((1, 512, 256), BF16), pltpu....]
where the time goes in v3:
time: 49.4 us; the launch traced here: 49.3 us
  Pallas kernels  48.6 us (98%)
  between operations  0.64 us (1%)
    pallas_call x1, Pallas kernels, per_device(): pl.pallas_call(kernel, out_shape=(pltpu.VMEM((1, 512, 256), BF16), pltpu....  47.9 us

profile of v3, /device:TPU:0, one launch (start us, length us, event | category | flops | bytes accessed | tf_op | source)
XLA Modules:
  0.0 49.3 jit_solution(17548735318761666096)
XLA Ops:
  0.6 47.9 %shard_map.85 = (bf16[1,512,256]{2,1,0:T(8,128)(2,1)S(1)}, f32[2,32,256]{2,1,0:T(8,128)S(1)}, f32[2,32,256]{2,1,0:T(8,128)S(1)}) custom-call(s32[2,8]{1,0:T(2,128)} %lengths.1, s32[16]{0:T(128)} %fold.1, bf16[1,512,256]{2,1,0:T(8,128)(2,1)} %q_hbm.1, bf16[2,512,256]{2,1,0:T(8,128)(2,1)} %k_hbm.1, bf16[2,512,256]{2,1,0:T(8,128)(2,1)} %v_hbm.1, ...), custom_call_target="tpu_custom_call" | custom-call | tf_op jit(solution)/shard_map/pallas_call | solution.py:397
  48.5 0.8 %shard_map.86 = (bf16[1,512,256]{2,1,0:T(8,128)(2,1)}, f32[2,32,256]{2,1,0:T(8,128)}, f32[2,32,256]{2,1,0:T(8,128)}) custom-call(bf16[1,512,256]{2,1,0:T(8,128)(2,1)S(1)} %get-tuple-element.6.a, f32[2,32,256]{2,1,0:T(8,128)S(1)} %get-tuple-element.7.b, f32[2,32,256]{2,1,0:T(8,128)S(1)} %get-tuple-element.8.c), custom_call_target="tpu_custom_call" | custom-call | tf_op jit(solution)/shard_map/pallas_call | solution.py:443

commit v4 on v3

--- a/solution.py
+++ b/solution.py
@@ -12,7 +12,8 @@
 F32 = jnp.float32
 BF16 = jnp.bfloat16
 ROW_HEADS = 8
-COPIES = 112
+COPIES = 71
+SENDS = 40
 LOW = 256
 
 
@@ -77,8 +78,10 @@
 
     def send(src, dst, device):
         i = len(started)
+        if i >= SENDS:
+            started[i - SENDS].wait_send()
         cp = pltpu.make_async_remote_copy(
-            src_ref=src, dst_ref=dst, send_sem=send_sem.at[i], recv_sem=recv_sem.at[i],
+            src_ref=src, dst_ref=dst, send_sem=send_sem.at[i % SENDS], recv_sem=recv_sem.at[i],
             device_id=device, device_id_type=MESH,
         )
         cp.start()
@@ -101,9 +104,6 @@
     v_p = same(vquarter(y, z, 0, 128), yp)
     v_m = same(vquarter(y, z, 0, 128), ym)
     v_f = same(vquarter(y, z, 0, 128), yf)
-    loads[1].wait()
-    ka_p = same(kv.at[y, 0, low], yp)
-    kb_m = same(kv.at[y, 0, high], ym)
     loads[2].wait()
     q_pair = same(qv.at[mine], partner)
     loads[3].wait()
@@ -133,10 +133,11 @@
 
     parts = [pl.ds(half * BLOCK, BLOCK) for half in (0, 1)]
 
-    def scores(j):
+    def scores(j, halves=(0, 1)):
         yi = chip(offsets[j])
         m = stat[0:1, :]
-        for half, part in enumerate(parts):
+        for half in halves:
+            part = parts[half]
             base = fold[4 * yi + 2 * c + half] * BLOCK
             raw = nn(kv[yi, 0, part, :], qst[...])
             ok = (rows >= first - base) & (rows <= pos - base)
@@ -175,6 +176,10 @@
         shares[k][1].wait_recv()
         relays[k] = a, same(vquarter(chip(k), around(z, 1), 64, 64), zm)
 
+    loads[1].wait()
+    ka_p = same(kv.at[y, 0, low], yp)
+    kb_m = same(kv.at[y, 0, high], ym)
+    scores(3)
     v_p.wait_recv()
     share(-1)
     v_m.wait_recv()
@@ -183,19 +188,20 @@
     ka_m = same(kv.at[y, 0, low], ym)
     v_f.wait_recv()
     share(2)
+    probs(3)
     ka_p.wait_recv()
     k2a = same(kv.at[chip(-1), 0, low], yp)
     kb_m.wait_recv()
     k2b = same(kv.at[chip(1), 0, high], ym)
-    scores(3)
-    probs(3)
     relay(-1)
+    scores(2, (0,))
     relay(1)
+    scores(1, (1,))
+    relay(2)
     kb_p.wait_recv()
+    scores(2, (1,))
     ka_m.wait_recv()
-    scores(1)
-    relay(2)
-    scores(2)
+    scores(1, (0,))
     for k in (-1, 1):
         for r in relays[k]:
             r.wait_recv()
@@ -298,10 +304,8 @@
     block(0)
     block(1)
     block(2)
+    block(3)
     values_second(0)
-    block(3)
-    values_early()
-    values_second(1)
     kc[1].wait_recv()
     ak[1, :, 0:2] = (up(ak[1, :, 0:2]) + up(rk[0])).astype(BF16)
     kc[14] = send(ak.at[1, far, lo], dk2.at[0, 0], diag[1, 1])
@@ -310,6 +314,8 @@
     ak[2, :, 2:4] = (up(ak[2, :, 2:4]) + up(rk[1])).astype(BF16)
     kc[16] = send(ak.at[2, far, hi], dk2.at[1, 0], diag[-1, -1])
     kc[6] = send(ak.at[2, near, hi], fk.at[1, pl.ds(0, 3), hi], ym)
+    values_second(1)
+    values_early()
     values_second(2)
     values_second(3)
 
@@ -358,14 +364,14 @@
         cp.wait_recv()
     xs[1] = (w + up(fev[0]) + up(fev[1])).astype(BF16)
     xc = []
-    for k in (1, 2, 3):
+    for k in (2, 1, 3):
         xc.append(send(xs.at[1, around(x, k)], rx.at[1, x], xo[k - 1]))
     dq_pair.wait_recv()
     dq_out[0] = ((jnp.transpose(dqt[:, mine]) + dqr[...]) * 0.0625).astype(BF16)
     for cp in gc.values():
         cp.wait_recv()
     xs[0] = (keys_along_y(1) + up(fgk[0]) + up(fgk[1])).astype(BF16)
-    for k in (1, 2, 3):
+    for k in (2, 1, 3):
         xc.append(send(xs.at[0, around(x, k)], rx.at[0, x], xo[k - 1]))
     rx[0, x] = xs[0, x]
     rx[1, x] = xs[1, x]
@@ -374,8 +380,9 @@
     for r in (0, 1):
         dk_out[r] = up(rx[0, 2 * r]) + up(rx[0, 2 * r + 1])
         dv_out[r] = up(rx[1, 2 * r]) + up(rx[1, 2 * r + 1])
-    for cp in started:
+    for cp in started[-SENDS:]:
         cp.wait_send()
+    assert len(started) == COPIES, len(started)
 
 
 def leave(a, b, c, a_out, b_out, c_out, sem):
@@ -433,7 +440,7 @@
             vm(2, 4, 32, 256),
             vm(2, 4, 32, 256),
             pltpu.SemaphoreType.DMA((4,)),
-            pltpu.SemaphoreType.DMA((COPIES,)),
+            pltpu.SemaphoreType.DMA((SENDS,)),
             pltpu.SemaphoreType.DMA((COPIES,)),
         ],
         compiler_params=pltpu.CompilerParams(

time: 49.4 us -> 47.4 us (0.960)
  Pallas kernels: 48.6 us -> 46.6 us
    pallas_call x1, Pallas kernels: 47.9 us -> 45.9 us  [per_device(): pl.pallas_call(kernel, out_shape=(pltpu.VMEM((1, 512, 256), BF16), pltpu....]
where the time goes in v4:
time: 47.4 us; the launch traced here: 47.3 us
  Pallas kernels  46.6 us (98%)
  between operations  0.64 us (1%)
    pallas_call x1, Pallas kernels, per_device(): pl.pallas_call(kernel, out_shape=(pltpu.VMEM((1, 512, 256), BF16), pltpu....  45.9 us

profile of v4, /device:TPU:0, one launch (start us, length us, event | category | flops | bytes accessed | tf_op | source)
XLA Modules:
  0.0 47.3 jit_solution(17968753331384544680)
XLA Ops:
  0.6 45.9 %shard_map.85 = (bf16[1,512,256]{2,1,0:T(8,128)(2,1)S(1)}, f32[2,32,256]{2,1,0:T(8,128)S(1)}, f32[2,32,256]{2,1,0:T(8,128)S(1)}) custom-call(s32[2,8]{1,0:T(2,128)} %lengths.1, s32[16]{0:T(128)} %fold.1, bf16[1,512,256]{2,1,0:T(8,128)(2,1)} %q_hbm.1, bf16[2,512,256]{2,1,0:T(8,128)(2,1)} %k_hbm.1, bf16[2,512,256]{2,1,0:T(8,128)(2,1)} %v_hbm.1, ...), custom_call_target="tpu_custom_call" | custom-call | tf_op jit(solution)/shard_map/pallas_call | solution.py:404
  46.5 0.8 %shard_map.86 = (bf16[1,512,256]{2,1,0:T(8,128)(2,1)}, f32[2,32,256]{2,1,0:T(8,128)}, f32[2,32,256]{2,1,0:T(8,128)}) custom-call(bf16[1,512,256]{2,1,0:T(8,128)(2,1)S(1)} %get-tuple-element.6.a, f32[2,32,256]{2,1,0:T(8,128)S(1)} %get-tuple-element.7.b, f32[2,32,256]{2,1,0:T(8,128)S(1)} %get-tuple-element.8.c), custom_call_target="tpu_custom_call" | custom-call | tf_op jit(solution)/shard_map/pallas_call | solution.py:450

commit v5 on v4

--- a/solution.py
+++ b/solution.py
@@ -12,9 +12,8 @@
 F32 = jnp.float32
 BF16 = jnp.bfloat16
 ROW_HEADS = 8
-COPIES = 71
+COPIES = 78
 SENDS = 40
-LOW = 256
 
 
 def nt(a, b):
@@ -99,7 +98,13 @@
     def vquarter(yi, zi, lo, n):
         return kv.at[yi, 1, pl.ds(pl.multiple_of(128 * zi + lo, 64), n)]
 
-    low, high = pl.ds(0, LOW), pl.ds(LOW, 512 - LOW)
+    low, high = pl.ds(0, 128), pl.ds(128, 128)
+    xb = lax.rem(x, 2)
+    xpair = {"seq": s, "head": 4 * (x + 1 - 2 * xb) + z}
+
+    def khalf(yi, lo, n):
+        return kv.at[yi, 0, pl.ds(pl.multiple_of(256 + 128 * xb + lo, 64), n)]
+
     loads[0].wait()
     v_p = same(vquarter(y, z, 0, 128), yp)
     v_m = same(vquarter(y, z, 0, 128), ym)
@@ -177,6 +182,8 @@
         relays[k] = a, same(vquarter(chip(k), around(z, 1), 64, 64), zm)
 
     loads[1].wait()
+    kx_p = same(khalf(y, 0, 128), yp)
+    kx_m = same(khalf(y, 0, 128), ym)
     ka_p = same(kv.at[y, 0, low], yp)
     kb_m = same(kv.at[y, 0, high], ym)
     scores(3)
@@ -189,27 +196,41 @@
     v_f.wait_recv()
     share(2)
     probs(3)
+    cross = {}
+    kx_p.wait_recv()
+    x2a = same(khalf(chip(-1), 0, 64), yp)
+    cross[-1] = same(khalf(chip(-1), 0, 128), xpair)
+    kx_m.wait_recv()
+    x2b = same(khalf(chip(1), 64, 64), ym)
+    cross[1] = same(khalf(chip(1), 0, 128), xpair)
     ka_p.wait_recv()
     k2a = same(kv.at[chip(-1), 0, low], yp)
     kb_m.wait_recv()
     k2b = same(kv.at[chip(1), 0, high], ym)
     relay(-1)
+    relay(1)
+    kb_p.wait_recv()
     scores(2, (0,))
-    relay(1)
-    scores(1, (1,))
+    x2a.wait_recv()
+    x2b.wait_recv()
+    cross[2] = same(khalf(chip(2), 0, 128), xpair)
     relay(2)
-    kb_p.wait_recv()
-    scores(2, (1,))
     ka_m.wait_recv()
     scores(1, (0,))
+    cross[-1].wait_recv()
+    scores(2, (1,))
+    cross[1].wait_recv()
+    scores(1, (1,))
+    k2a.wait_recv()
+    k2b.wait_recv()
+    scores(0, (0,))
     for k in (-1, 1):
         for r in relays[k]:
             r.wait_recv()
     probs(1)
     probs(2)
-    k2a.wait_recv()
-    k2b.wait_recv()
-    scores(0)
+    cross[2].wait_recv()
+    scores(0, (1,))
     for r in relays[2]:
         r.wait_recv()
     probs(0)

time: 47.4 us -> 47.1 us (level)
  no operation moved by 1% of the time
where the time goes in v5:
time: 47.1 us; the launch traced here: 47 us
  Pallas kernels  46.3 us (98%)
  between operations  0.64 us (1%)
    pallas_call x1, Pallas kernels, per_device(): pl.pallas_call(kernel, out_shape=(pltpu.VMEM((1, 512, 256), BF16), pltpu....  45.6 us

profile of v5, /device:TPU:0, one launch (start us, length us, event | category | flops | bytes accessed | tf_op | source)
XLA Modules:
  0.0 47.0 jit_solution(6274585324473859520)
XLA Ops:
  0.6 45.6 %shard_map.85 = (bf16[1,512,256]{2,1,0:T(8,128)(2,1)S(1)}, f32[2,32,256]{2,1,0:T(8,128)S(1)}, f32[2,32,256]{2,1,0:T(8,128)S(1)}) custom-call(s32[2,8]{1,0:T(2,128)} %lengths.1, s32[16]{0:T(128)} %fold.1, bf16[1,512,256]{2,1,0:T(8,128)(2,1)} %q_hbm.1, bf16[2,512,256]{2,1,0:T(8,128)(2,1)} %k_hbm.1, bf16[2,512,256]{2,1,0:T(8,128)(2,1)} %v_hbm.1, ...), custom_call_target="tpu_custom_call" | custom-call | tf_op jit(solution)/shard_map/pallas_call | solution.py:425
  46.2 0.8 %shard_map.86 = (bf16[1,512,256]{2,1,0:T(8,128)(2,1)}, f32[2,32,256]{2,1,0:T(8,128)}, f32[2,32,256]{2,1,0:T(8,128)}) custom-call(bf16[1,512,256]{2,1,0:T(8,128)(2,1)S(1)} %get-tuple-element.6.a, f32[2,32,256]{2,1,0:T(8,128)S(1)} %get-tuple-element.7.b, f32[2,32,256]{2,1,0:T(8,128)S(1)} %get-tuple-element.8.c), custom_call_target="tpu_custom_call" | custom-call | tf_op jit(solution)/shard_map/pallas_call | solution.py:471

commit v6 on v5

--- a/solution.py
+++ b/solution.py
@@ -138,18 +138,15 @@
 
     parts = [pl.ds(half * BLOCK, BLOCK) for half in (0, 1)]
 
-    def scores(j, halves=(0, 1)):
+    def scores(j, half, off=0, n=BLOCK):
         yi = chip(offsets[j])
-        m = stat[0:1, :]
-        for half in halves:
-            part = parts[half]
-            base = fold[4 * yi + 2 * c + half] * BLOCK
-            raw = nn(kv[yi, 0, part, :], qst[...])
-            ok = (rows >= first - base) & (rows <= pos - base)
-            s2 = jnp.where(ok, raw * LOG2E, MASKED)
-            sc[j, part, :] = s2
-            m = jnp.maximum(m, jnp.max(s2, axis=0, keepdims=True))
-        stat[0:1, :] = m
+        part = pl.ds(pl.multiple_of(half * BLOCK + off, 128), n)
+        base = fold[4 * yi + 2 * c + half] * BLOCK + off
+        raw = nn(kv[yi, 0, part, :], qst[...])
+        ok = (rows[:n] >= first - base) & (rows[:n] <= pos - base)
+        s2 = jnp.where(ok, raw * LOG2E, MASKED)
+        sc[j, part, :] = s2
+        stat[0:1, :] = jnp.maximum(stat[0:1, :], jnp.max(s2, axis=0, keepdims=True))
 
     def probs(j):
         yi = chip(offsets[j])
@@ -186,7 +183,8 @@
     kx_m = same(khalf(y, 0, 128), ym)
     ka_p = same(kv.at[y, 0, low], yp)
     kb_m = same(kv.at[y, 0, high], ym)
-    scores(3)
+    scores(3, 0)
+    scores(3, 1)
     v_p.wait_recv()
     share(-1)
     v_m.wait_recv()
@@ -203,34 +201,39 @@
     kx_m.wait_recv()
     x2b = same(khalf(chip(1), 64, 64), ym)
     cross[1] = same(khalf(chip(1), 0, 128), xpair)
+    scores(2, 1, 128 * xb, 128)
+    scores(1, 1, 128 * xb, 128)
     ka_p.wait_recv()
     k2a = same(kv.at[chip(-1), 0, low], yp)
     kb_m.wait_recv()
     k2b = same(kv.at[chip(1), 0, high], ym)
+    scores(2, 0, 0, 128)
     relay(-1)
+    scores(1, 0, 128, 128)
     relay(1)
     kb_p.wait_recv()
-    scores(2, (0,))
+    scores(2, 0, 128, 128)
     x2a.wait_recv()
     x2b.wait_recv()
     cross[2] = same(khalf(chip(2), 0, 128), xpair)
     relay(2)
     ka_m.wait_recv()
-    scores(1, (0,))
+    scores(1, 0, 0, 128)
     cross[-1].wait_recv()
-    scores(2, (1,))
+    scores(2, 1, 128 * (1 - xb), 128)
     cross[1].wait_recv()
-    scores(1, (1,))
+    scores(1, 1, 128 * (1 - xb), 128)
     k2a.wait_recv()
     k2b.wait_recv()
-    scores(0, (0,))
-    for k in (-1, 1):
-        for r in relays[k]:
-            r.wait_recv()
+    scores(0, 0)
+    for r in relays[-1]:
+        r.wait_recv()
+    probs(2)
+    for r in relays[1]:
+        r.wait_recv()
     probs(1)
-    probs(2)
     cross[2].wait_recv()
-    scores(0, (1,))
+    scores(0, 1)
     for r in relays[2]:
         r.wait_recv()
     probs(0)

time: 47.1 us -> 46.7 us (level)
  no operation moved by 1% of the time
where the time goes in v6:
time: 46.7 us; the launch traced here: 46.6 us
  Pallas kernels  46 us (99%)
  between operations  0.64 us (1%)
    pallas_call x1, Pallas kernels, per_device(): pl.pallas_call(kernel, out_shape=(pltpu.VMEM((1, 512, 256), BF16), pltpu....  45.2 us

profile of v6, /device:TPU:0, one launch (start us, length us, event | category | flops | bytes accessed | tf_op | source)
XLA Modules:
  0.0 46.6 jit_solution(10915505297250121429)
XLA Ops:
  0.6 45.2 %shard_map.85 = (bf16[1,512,256]{2,1,0:T(8,128)(2,1)S(1)}, f32[2,32,256]{2,1,0:T(8,128)S(1)}, f32[2,32,256]{2,1,0:T(8,128)S(1)}) custom-call(s32[2,8]{1,0:T(2,128)} %lengths.1, s32[16]{0:T(128)} %fold.1, bf16[1,512,256]{2,1,0:T(8,128)(2,1)} %q_hbm.1, bf16[2,512,256]{2,1,0:T(8,128)(2,1)} %k_hbm.1, bf16[2,512,256]{2,1,0:T(8,128)(2,1)} %v_hbm.1, ...), custom_call_target="tpu_custom_call" | custom-call | tf_op jit(solution)/shard_map/pallas_call | solution.py:428
  45.8 0.8 %shard_map.86 = (bf16[1,512,256]{2,1,0:T(8,128)(2,1)}, f32[2,32,256]{2,1,0:T(8,128)}, f32[2,32,256]{2,1,0:T(8,128)}) custom-call(bf16[1,512,256]{2,1,0:T(8,128)(2,1)S(1)} %get-tuple-element.6.a, f32[2,32,256]{2,1,0:T(8,128)S(1)} %get-tuple-element.7.b, f32[2,32,256]{2,1,0:T(8,128)S(1)} %get-tuple-element.8.c), custom_call_target="tpu_custom_call" | custom-call | tf_op jit(solution)/shard_map/pallas_call | solution.py:474

commit v7 on v6

--- a/solution.py
+++ b/solution.py
@@ -12,8 +12,8 @@
 F32 = jnp.float32
 BF16 = jnp.bfloat16
 ROW_HEADS = 8
-COPIES = 78
-SENDS = 40
+COPIES = 63
+SENDS = 32
 
 
 def nt(a, b):
@@ -75,17 +75,29 @@
 
     started = []
 
-    def send(src, dst, device):
+    used = [0]
+
+    def take():
+        used[0] += 1
+        return used[0] - 1
+
+    def remote(src, dst, device, i, r):
+        return pltpu.make_async_remote_copy(
+            src_ref=src, dst_ref=dst, send_sem=send_sem.at[i], recv_sem=recv_sem.at[r],
+            device_id=device, device_id_type=MESH,
+        )
+
+    def send(src, dst, device, group=None):
         i = len(started)
         if i >= SENDS:
             started[i - SENDS].wait_send()
-        cp = pltpu.make_async_remote_copy(
-            src_ref=src, dst_ref=dst, send_sem=send_sem.at[i % SENDS], recv_sem=recv_sem.at[i],
-            device_id=device, device_id_type=MESH,
-        )
+        cp = remote(src, dst, device, i % SENDS, take() if group is None else group)
         cp.start()
         started.append(cp)
         return cp
+
+    def wait_group(whole, group):
+        remote(whole, whole, partner, 0, group).wait_recv()
 
     def same(ref, device):
         return send(ref, ref, device)
@@ -271,36 +283,38 @@
     lo, hi = pl.ds(0, 2), pl.ds(2, 2)
     near, far = pl.ds(0, 3), 3
     kc, vc = {}, {}
+    vgroup = [take() for _ in range(4)]
+    kgroup = take()
 
     def values_second(j):
         vc[j, 1].wait_recv()
         av[j, 2, 0:2] = (up(av[j, 2, 0:2]) + up(rv[0, j])).astype(BF16)
         if j == 0:
-            vc[j, 4] = send(av.at[j, 2, lo], dv2.at[0, 0], diag[1, 1])
+            vc[j, 4] = send(av.at[j, 2, lo], dv2.at[0, 0], diag[1, 1], vgroup[0])
         else:
-            vc[j, 4] = send(av.at[j, 2, lo], fv.at[0, j, lo], zp)
+            vc[j, 4] = send(av.at[j, 2, lo], fv.at[0, j, lo], zp, vgroup[j])
         vc[j, 2].wait_recv()
         av[j, 0, 2:4] = (up(av[j, 0, 2:4]) + up(rv[1, j])).astype(BF16)
         if j == 0:
-            vc[j, 6] = send(av.at[j, 0, hi], dv2.at[1, 0], diag[-1, -1])
+            vc[j, 6] = send(av.at[j, 0, hi], dv2.at[1, 0], diag[-1, -1], vgroup[0])
         else:
-            vc[j, 6] = send(av.at[j, 0, hi], fv.at[1, j, hi], zm)
+            vc[j, 6] = send(av.at[j, 0, hi], fv.at[1, j, hi], zm, vgroup[j])
 
     def values_early():
         vc[0, 5].wait_recv()
         av[0, 1, 0:2] = (up(av[0, 1, 0:2]) + up(fv[1, 0, 0:2])).astype(BF16)
-        vc[0, 7] = send(av.at[0, 1, lo], dv2.at[0, 1], yp)
+        vc[0, 7] = send(av.at[0, 1, lo], dv2.at[0, 1], yp, vgroup[0])
         vc[0, 3].wait_recv()
         av[0, 1, 2:4] = (up(av[0, 1, 2:4]) + up(fv[0, 0, 2:4])).astype(BF16)
-        vc[0, 8] = send(av.at[0, 1, hi], dv2.at[1, 1], ym)
+        vc[0, 8] = send(av.at[0, 1, hi], dv2.at[1, 1], ym, vgroup[0])
 
     def keys_early():
         kc[5].wait_recv()
         ak[3, 3, 0:2] = (up(ak[3, 3, 0:2]) + up(fk[1, 3, 0:2])).astype(BF16)
-        kc[17] = send(ak.at[3, far, lo], dk2.at[0, 1], zp)
+        kc[17] = send(ak.at[3, far, lo], dk2.at[0, 1], zp, kgroup)
         kc[3].wait_recv()
         ak[3, 3, 2:4] = (up(ak[3, 3, 2:4]) + up(fk[0, 3, 2:4])).astype(BF16)
-        kc[18] = send(ak.at[3, far, hi], dk2.at[1, 1], zm)
+        kc[18] = send(ak.at[3, far, hi], dk2.at[1, 1], zm, kgroup)
 
     def block(j):
         for half, (gk_, gv) in enumerate(backward(j)):
@@ -321,9 +335,9 @@
             if j == 2 and half == 0:
                 kc[5] = send(ak.at[2, pl.ds(0, 4), lo], fk.at[1, pl.ds(0, 4), lo], ym)
             if half == 0:
-                vc[j, 5] = send(av.at[j, 0, lo], fv.at[1, j, lo], zm)
+                vc[j, 5] = send(av.at[j, 0, lo], fv.at[1, j, lo], zm, vgroup[j] if j else None)
             else:
-                vc[j, 3] = send(av.at[j, 2, hi], fv.at[0, j, hi], zp)
+                vc[j, 3] = send(av.at[j, 2, hi], fv.at[0, j, hi], zp, vgroup[j] if j else None)
 
     block(0)
     block(1)
@@ -332,11 +346,11 @@
     values_second(0)
     kc[1].wait_recv()
     ak[1, :, 0:2] = (up(ak[1, :, 0:2]) + up(rk[0])).astype(BF16)
-    kc[14] = send(ak.at[1, far, lo], dk2.at[0, 0], diag[1, 1])
+    kc[14] = send(ak.at[1, far, lo], dk2.at[0, 0], diag[1, 1], kgroup)
     kc[4] = send(ak.at[1, near, lo], fk.at[0, pl.ds(0, 3), lo], yp)
     kc[2].wait_recv()
     ak[2, :, 2:4] = (up(ak[2, :, 2:4]) + up(rk[1])).astype(BF16)
-    kc[16] = send(ak.at[2, far, hi], dk2.at[1, 0], diag[-1, -1])
+    kc[16] = send(ak.at[2, far, hi], dk2.at[1, 0], diag[-1, -1], kgroup)
     kc[6] = send(ak.at[2, near, hi], fk.at[1, pl.ds(0, 3), hi], ym)
     values_second(1)
     values_early()
@@ -349,12 +363,10 @@
     dq_pair = send(dqs, dqr, partner)
 
     def values_along_z(j):
-        for i in (3, 4, 5, 6):
-            vc[j, i].wait_recv()
+        wait_group(fv.at[pl.ds(0, 2), j], vgroup[j])
         return up(av[j, 1]) + up(fv[0, j]) + up(fv[1, j])
 
-    for i in (4, 6, 7, 8):
-        vc[0, i].wait_recv()
+    wait_group(dv2, vgroup[0])
     ec = {}
     w = values_along_z(1)
     zv[0, 0:2] = (w[0:2] + up(dv2[0, 0]) + up(dv2[0, 1])).astype(BF16)
@@ -371,8 +383,7 @@
     def keys_along_y(q):
         return up(ak[3, q]) + up(fk[0, q]) + up(fk[1, q])
 
-    for i in (14, 16, 17, 18):
-        kc[i].wait_recv()
+    wait_group(dk2, kgroup)
     gc = {}
     w = keys_along_y(2)
     yk[0, 0:2] = (w[0:2] + up(dk2[0, 0]) + up(dk2[0, 1])).astype(BF16)
@@ -406,7 +417,7 @@
         dv_out[r] = up(rx[1, 2 * r]) + up(rx[1, 2 * r + 1])
     for cp in started[-SENDS:]:
         cp.wait_send()
-    assert len(started) == COPIES, len(started)
+    assert used[0] == COPIES, used[0]
 
 
 def leave(a, b, c, a_out, b_out, c_out, sem):

time: 46.7 us -> 46.5 us (level)
  no operation moved by 1% of the time
where the time goes in v7:
time: 46.5 us; the launch traced here: 46.4 us
  Pallas kernels  45.7 us (98%)
  between operations  0.64 us (1%)
    pallas_call x1, Pallas kernels, per_device(): pl.pallas_call(kernel, out_shape=(pltpu.VMEM((1, 512, 256), BF16), pltpu....  45 us

profile of v7, /device:TPU:0, one launch (start us, length us, event | category | flops | bytes accessed | tf_op | source)
XLA Modules:
  0.0 46.4 jit_solution(16550199184078766214)
XLA Ops:
  0.6 45.0 %shard_map.85 = (bf16[1,512,256]{2,1,0:T(8,128)(2,1)S(1)}, f32[2,32,256]{2,1,0:T(8,128)S(1)}, f32[2,32,256]{2,1,0:T(8,128)S(1)}) custom-call(s32[2,8]{1,0:T(2,128)} %lengths.1, s32[16]{0:T(128)} %fold.1, bf16[1,512,256]{2,1,0:T(8,128)(2,1)} %q_hbm.1, bf16[2,512,256]{2,1,0:T(8,128)(2,1)} %k_hbm.1, bf16[2,512,256]{2,1,0:T(8,128)(2,1)} %v_hbm.1, ...), custom_call_target="tpu_custom_call" | custom-call | tf_op jit(solution)/shard_map/pallas_call | solution.py:439
  45.6 0.8 %shard_map.86 = (bf16[1,512,256]{2,1,0:T(8,128)(2,1)}, f32[2,32,256]{2,1,0:T(8,128)}, f32[2,32,256]{2,1,0:T(8,128)}) custom-call(bf16[1,512,256]{2,1,0:T(8,128)(2,1)S(1)} %get-tuple-element.6.a, f32[2,32,256]{2,1,0:T(8,128)S(1)} %get-tuple-element.7.b, f32[2,32,256]{2,1,0:T(8,128)S(1)} %get-tuple-element.8.c), custom_call_target="tpu_custom_call" | custom-call | tf_op jit(solution)/shard_map/pallas_call | solution.py:485

commit v8 on v6

--- a/solution.py
+++ b/solution.py
@@ -154,9 +154,9 @@
         alpha = jnp.exp2(stat[3:4, :] - m)
         total = stat[1:2, :] * alpha
         dot = stat[2:3, :] * alpha
+        dp[j] = nn(kv[yi, 1], dot_[...])
         for part in parts:
-            gp = nn(kv[yi, 1, part, :], dot_[...])
-            dp[j, part, :] = gp
+            gp = dp[j, part, :]
             e = jnp.exp2(sc[j, part, :] - m)
             total = total + jnp.sum(e, axis=0, keepdims=True)
             dot = dot + jnp.sum(e * gp, axis=0, keepdims=True)
@@ -248,14 +248,10 @@
     gdot = (stat[2:3, :] * w1 + stat2[2:3, :] * w2) / total
 
     def backward(j):
-        out = []
-        for half in (0, 1):
-            part = pl.ds(half * BLOCK, BLOCK)
-            p = jnp.exp2(sc[j, part, :] - lse)
-            ds = (p * (dp[j, part, :] - gdot)).astype(BF16)
-            dsb[j, part, :] = ds
-            out.append((nn(ds, qs[...]), nn(p.astype(BF16), dov[...])))
-        return out
+        p = jnp.exp2(sc[j] - lse)
+        ds = (p * (dp[j] - gdot)).astype(BF16)
+        dsb[j] = ds
+        return nn(ds, qs[...]), nn(p.astype(BF16), dov[...])
 
     def queries():
         acc = tn(kv[chip(offsets[0]), 0], dsb[0])
@@ -303,13 +299,12 @@
         kc[18] = send(ak.at[3, far, hi], dk2.at[1, 1], zm)
 
     def block(j):
-        for half, (gk_, gv) in enumerate(backward(j)):
-            gk_, gv = gk_.astype(BF16), gv.astype(BF16)
-            for xp, zi in pieces:
-                r0 = (4 * xp + zi) * 32 - half * BLOCK
-                if 0 <= r0 < BLOCK:
-                    ak[j, place[zi], xp] = gk_[r0 : r0 + 32, :]
-                    av[j, place[zi], xp] = gv[r0 : r0 + 32, :]
+        gk_, gv = backward(j)
+        gk_, gv = gk_.astype(BF16), gv.astype(BF16)
+        for xp, zi in pieces:
+            r0 = (4 * xp + zi) * 32
+            ak[j, place[zi], xp] = gk_[r0 : r0 + 32, :]
+            av[j, place[zi], xp] = gv[r0 : r0 + 32, :]
         for half in (0, 1):
             at_ = (lo, hi)[half]
             to = (zp, zm)[half]

time: 46.7 us -> 46.7 us (level)
  no operation moved by 1% of the time
where the time goes in v8:
time: 46.7 us; the launch traced here: 46.6 us
  Pallas kernels  46 us (99%)
  between operations  0.64 us (1%)
    pallas_call x1, Pallas kernels, per_device(): pl.pallas_call(kernel, out_shape=(pltpu.VMEM((1, 512, 256), BF16), pltpu....  45.2 us

profile of v8, /device:TPU:0, one launch (start us, length us, event | category | flops | bytes accessed | tf_op | source)
XLA Modules:
  0.0 46.6 jit_solution(5545476424262635263)
XLA Ops:
  0.6 45.2 %shard_map.85 = (bf16[1,512,256]{2,1,0:T(8,128)(2,1)S(1)}, f32[2,32,256]{2,1,0:T(8,128)S(1)}, f32[2,32,256]{2,1,0:T(8,128)S(1)}) custom-call(s32[2,8]{1,0:T(2,128)} %lengths.1, s32[16]{0:T(128)} %fold.1, bf16[1,512,256]{2,1,0:T(8,128)(2,1)} %q_hbm.1, bf16[2,512,256]{2,1,0:T(8,128)(2,1)} %k_hbm.1, bf16[2,512,256]{2,1,0:T(8,128)(2,1)} %v_hbm.1, ...), custom_call_target="tpu_custom_call" | custom-call | tf_op jit(solution)/shard_map/pallas_call | solution.py:423
  45.8 0.8 %shard_map.86 = (bf16[1,512,256]{2,1,0:T(8,128)(2,1)}, f32[2,32,256]{2,1,0:T(8,128)}, f32[2,32,256]{2,1,0:T(8,128)}) custom-call(bf16[1,512,256]{2,1,0:T(8,128)(2,1)S(1)} %get-tuple-element.6.a, f32[2,32,256]{2,1,0:T(8,128)S(1)} %get-tuple-element.7.b, f32[2,32,256]{2,1,0:T(8,128)S(1)} %get-tuple-element.8.c), custom_call_target="tpu_custom_call" | custom-call | tf_op jit(solution)/shard_map/pallas_call | solution.py:469
